TPU v7x, 8 devices: a whole 2x2x1 slice. The times are simulated.
8 devices in a mesh: dp: 1 (over z), pool: 2 (over y), ep: 4 (over x, core).
Axes of the slice: x: 2, y: 2, z: 1, core: 2. Of those that a mesh axis runs over, the one named last changes fastest.
Arguments:
- hidden_in: bfloat16 [512, 1024], P(('dp', 'ep'))
- k_cache: bfloat16 [2, 512, 128, 8, 128], P(None, ('dp', 'ep'), 'pool')
- v_cache: bfloat16 [2, 512, 128, 8, 128], P(None, ('dp', 'ep'), 'pool')
- cache_len: int32 [512], P(('dp', 'ep'))
- w_q: bfloat16 [2, 1024, 1024], replicated
- w_k: bfloat16 [2, 1024, 1024], replicated
- w_v: bfloat16 [2, 1024, 1024], replicated
- w_o: bfloat16 [2, 1024, 1024], replicated
- w_router: float32 [2, 1024, 64], replicated
- expert_ids: int32 [2, 512, 6], P(None, ('dp', 'ep'))
- w_one: bfloat16 [2, 64, 1024, 704], P(None, 'ep', None, 'pool')
- w_three: bfloat16 [2, 64, 1024, 704], P(None, 'ep', None, 'pool')
- w_two: bfloat16 [2, 64, 704, 1024], P(None, 'ep', 'pool')
Outputs:
- output: bfloat16 [512, 1024], P(('dp', 'ep'))
All inputs are finite; a program needn't handle non-finite values.
Results may differ from a plain program's by a relative error of at most 0.02.
Values are sent between devices in bfloat16 or wider.
A program may use at most 1 GiB of HBM per device.

v0:
```python
import functools

import jax
import jax.numpy as jnp
from jax import lax
from jax.experimental import pallas as pl
from jax.experimental.pallas import tpu as pltpu
from jax.sharding import PartitionSpec as P


MESH = pl.DeviceIdType.MESH
F32 = jnp.float32
BF16 = jnp.bfloat16
I32 = jnp.int32
EPS = 1e-6
NEG = -1e30
TB = 8
SLOTS = 4
TILE_M = 128
PARTS = 3
DEPTH = 4
VMEM_MIB = (51, 51)


def _nn(a, b):
    return lax.dot_general(a, b, (((1,), (0,)), ((), ())), preferred_element_type=F32)


def _nt(a, b, precision=None):
    return lax.dot_general(a, b, (((1,), (1,)), ((), ())), preferred_element_type=F32, precision=precision)


def _rms(v):
    return v * lax.rsqrt(jnp.mean(v * v, axis=-1, keepdims=True) + EPS)


def _where_am_i():
    p = lax.axis_index("pool")
    b = lax.axis_index("ep")
    x, c = b // 2, b % 2
    to_y = {"pool": 1 - p}
    to_x = {"ep": (1 - x) * 2 + c}
    to_c = {"ep": x * 2 + (1 - c)}
    return p, b, x, c, to_y, to_x, to_c


def _greet(peers):
    sem = pltpu.get_barrier_semaphore()
    for peer in peers:
        pl.semaphore_signal(sem, inc=1, device_id=peer, device_id_type=MESH)
    pl.semaphore_wait(sem, len(peers))


def _rcopy(src, dst, send, recv, peer):
    return pltpu.make_async_remote_copy(src_ref=src, dst_ref=dst, send_sem=send, recv_sem=recv, device_id=peer, device_id_type=MESH)


def _route(b, idg, pos_out, ids_out, off_out):
    n_local, top_k = off_out.shape[1], 6
    n_tok = pos_out.shape[2]
    er = lax.broadcasted_iota(I32, (n_local, n_tok), 0)
    tri = (lax.broadcasted_iota(I32, (n_tok, n_tok), 0) <= lax.broadcasted_iota(I32, (n_tok, n_tok), 1)).astype(F32).astype(BF16)
    before = (lax.broadcasted_iota(I32, (n_local, n_local), 0) > lax.broadcasted_iota(I32, (n_local, n_local), 1)).astype(F32).astype(BF16)
    row = lax.broadcasted_iota(I32, (8, n_tok), 0)
    for layer in range(pos_out.shape[0]):
        ids = jnp.concatenate([idg[i, layer] for i in range(idg.shape[0])], axis=1)
        local = ids - b * n_local
        member = jnp.zeros((n_local, n_tok), F32)
        for k in range(top_k):
            member = member + jnp.where(er == local[k:k + 1, :], 1.0, 0.0)
        member = member.astype(BF16)
        cum = _nn(member, tri)
        first = jnp.sum(_nn(before, member), axis=1, keepdims=True)
        place = first + cum - 1.0
        pos = jnp.full((8, n_tok), -1.0, F32)
        for k in range(top_k):
            lk = local[k:k + 1, :]
            at = jnp.sum(jnp.where(er == lk, place, 0.0), axis=0, keepdims=True)
            at = jnp.where((lk >= 0) & (lk < n_local), at, -1.0)
            pos = jnp.where(row == k, at, pos)
        pos_out[layer] = pos.astype(I32)
        ids_out[layer] = ids
        off_out[layer] = jnp.broadcast_to(first, (n_local, 128)).astype(I32)


def attn_kernel(layer, routed, x_ref, len_ref, k_hbm, v_hbm, wq_hbm, wk_hbm, wv_hbm, wo_hbm, *refs):
    if routed:
        ids_ref, *refs = refs
    u_all, a_out, a_recv, *refs = refs
    if routed:
        pos_out, ids_out, off_out, *refs, idg, isend, irecv = refs
    (kbuf, vbuf, pbuf, wq, wk, wv, wo, q3, o3, o3r, k3, v3, mls, mlr, o2, a_own,
     ksem, vsem, wsem, osend, orecv, gsend, grecv) = refs
    p, b, x, c, to_y, to_x, to_c = _where_am_i()
    half = x_ref.shape[0] // 2
    heads, dim = q3.shape[1], q3.shape[2]
    rows = kbuf.shape[2]
    n_half = half // TB
    n_blocks = 2 * n_half
    scale = dim ** -0.5

    def tok_of(n):
        return ((1 - p) + (n // n_half) * (2 * p - 1)) * half + (n % n_half) * TB

    def kv_copies(n):
        slot = n % SLOTS
        src = pl.ds(tok_of(n), TB)
        return (pltpu.make_async_copy(k_hbm.at[layer, src], kbuf.at[slot], ksem.at[slot]),
                pltpu.make_async_copy(v_hbm.at[layer, src], vbuf.at[slot], vsem.at[slot]))

    w_copies = [pltpu.make_async_copy(src.at[layer], dst, wsem.at[i])
                for i, (src, dst) in enumerate(((wq_hbm, wq), (wk_hbm, wk), (wv_hbm, wv), (wo_hbm, wo)))]
    w_copies[0].start()
    for n in range(SLOTS):
        for cp in kv_copies(n):
            cp.start()
    for cp in w_copies[1:]:
        cp.start()

    if routed:
        to_d = {"ep": (1 - x) * 2 + (1 - c)}
        _greet((to_y, to_x, to_c, to_d))
        idg[b] = ids_ref[...]
        id_copies = [_rcopy(ids_ref, idg.at[b], isend.at[i], irecv.at[i], peer) for i, peer in enumerate((to_x, to_c, to_d))]
        for cp in id_copies:
            cp.start()
    else:
        _greet((to_y, to_x, to_c))

    normed = _rms(x_ref[...].astype(F32)).astype(BF16)
    w_copies[0].wait()
    for h in range(0, heads, 2):
        part = _nn(normed, wq[:, h * dim:(h + 2) * dim]).astype(BF16).astype(F32)
        q3[:, h, :] = part[:, :dim]
        q3[:, h + 1, :] = part[:, dim:]

    row_i = lax.broadcasted_iota(I32, (heads, rows), 0)
    lane_i = lax.broadcasted_iota(I32, (heads, rows), 1)
    posl = jnp.where(lane_i % heads == row_i, lane_i // heads + p * (rows // heads), 1 << 20)
    lane = lax.broadcasted_iota(I32, (heads, 128), 1)

    def block(n, acc):
        slot = n % SLOTS
        for cp in kv_copies(n):
            cp.wait()
        t0 = tok_of(n)

        def scores(_, acc):
            for j in range(TB):
                q = q3[t0 + j].astype(BF16)
                s = _nt(q, kbuf[slot, j])
                s = jnp.where(posl < len_ref[t0 + j], s * scale, NEG)
                m = jnp.max(s, axis=1, keepdims=True)
                pr = jnp.exp(s - m)
                l = jnp.sum(pr, axis=1, keepdims=True)
                pbuf[j] = pr.astype(BF16)
                at = (n % n_half) * TB + j
                acc = jnp.where(lane == at, m, acc)
                acc = jnp.where(lane == half + at, l, acc)
            return acc

        def values(_, none):
            for j in range(TB):
                o3[t0 + j] = _nn(pbuf[j], vbuf[slot, j])
            return none

        acc = lax.fori_loop(0, 1, scores, acc)
        lax.fori_loop(0, 1, values, 0)

        @pl.when(n + SLOTS < n_blocks)
        def _():
            for cp in kv_copies(n + SLOTS):
                cp.start()

        return acc

    theirs = (1 - p) * half
    mine = p * half

    def o_copy(i):
        return _rcopy(o3.at[pl.ds(theirs + i * TB, TB)], o3r.at[pl.ds(i * TB, TB)], osend.at[i], orecv.at[i], to_y)

    def first(n, acc):
        acc = block(n, acc)
        o_copy(n).start()
        return acc

    zero = jnp.zeros((heads, 128), F32)
    mls[...] = lax.fori_loop(0, n_half, first, zero)
    ml_copy = _rcopy(mls, mlr, osend.at[n_half], orecv.at[n_half], to_y)
    ml_copy.start()
    normed = _rms(x_ref[pl.ds(mine, half), :].astype(F32)).astype(BF16)
    for i, (w, dst) in enumerate(((wk, k3), (wv, v3))):
        w_copies[1 + i].wait()
        for h in range(0, heads, 2):
            part = _nn(normed, w[:, h * dim:(h + 2) * dim]).astype(BF16).astype(F32)
            dst[:, h, :] = part[:, :dim]
            dst[:, h + 1, :] = part[:, dim:]

    sn = zero
    for j in range(half):
        sn = jnp.where(lane == j, jnp.sum(q3[mine + j] * k3[j], axis=1, keepdims=True) * scale, sn)

    if routed:
        for cp in id_copies:
            cp.wait()
        _route(b, idg, pos_out, ids_out, off_out)

    ml_own = lax.fori_loop(n_half, n_blocks, block, zero)

    for i in range(n_half):
        o_copy(i).wait()
    ml_copy.wait()
    ml_their = mlr[...]
    top = jnp.maximum(jnp.maximum(ml_own, ml_their), sn)
    w_own, w_their, w_new = jnp.exp(ml_own - top), jnp.exp(ml_their - top), jnp.exp(sn - top)
    den = pltpu.roll(ml_own, half, 1) * w_own + pltpu.roll(ml_their, half, 1) * w_their + w_new
    w_own, w_their, w_new = w_own / den, w_their / den, w_new / den
    for j in range(half):
        o3r[j] = (o3[mine + j] * w_own[:, j:j + 1] + o3r[j] * w_their[:, j:j + 1] + v3[j] * w_new[:, j:j + 1])
    for h in range(heads):
        o2[:, h * dim:(h + 1) * dim] = o3r[:, h, :].astype(BF16)
    w_copies[3].wait()
    d_model = x_ref.shape[1]
    a = (x_ref[pl.ds(mine, half), :].astype(F32) + _nn(o2[...], wo[...])).astype(BF16)
    a_own[...] = a
    me = b * 2 + p
    u_all[me] = _rms(a.astype(F32)).astype(BF16)

    y_blk, x_blk = b * 2 + (1 - p), ((1 - x) * 2 + c) * 2 + p
    d_blk = ((1 - x) * 2 + c) * 2 + (1 - p)
    lo, hi = pl.ds(0, half // 2), pl.ds(half // 2, half // 2)

    def u_copy(i, src, peer, part=None):
        ref = u_all.at[src] if part is None else u_all.at[src, part]
        return _rcopy(ref, ref, gsend.at[i], grecv.at[i], peer)

    own_y = [u_copy(0, me, to_y, lo), u_copy(1, me, to_y, hi)]
    own_x = [u_copy(2, me, to_x, hi), u_copy(3, me, to_x, lo)]
    own_c = u_copy(4, me, to_c)
    for cp in (own_y[0], own_x[0], own_y[1], own_x[1], own_c):
        cp.start()
    cw = d_model // 2
    a_out[...] = a_own[:, pl.ds(pl.multiple_of(p * cw, 128), cw)]
    a_copy = _rcopy(a_own.at[:, pl.ds(pl.multiple_of((1 - p) * cw, 128), cw)], a_recv, gsend.at[10], grecv.at[10], to_y)
    own_y[0].wait_recv()
    fwd_x = u_copy(5, y_blk, to_x, lo)
    fwd_x.start()
    own_x[0].wait_recv()
    fwd_y = u_copy(6, x_blk, to_y, hi)
    fwd_y.start()
    a_copy.start()
    own_y[1].wait_recv()
    c_y = u_copy(7, y_blk, to_c)
    c_y.start()
    own_x[1].wait_recv()
    c_x = u_copy(8, x_blk, to_c)
    c_x.start()
    fwd_x.wait_recv()
    fwd_y.wait_recv()
    c_d = u_copy(9, d_blk, to_c)
    c_d.start()
    for cp in (own_c, c_y, c_x, c_d, a_copy):
        cp.wait_recv()
    for cp in (*own_y, *own_x, own_c, fwd_x, c_y, fwd_y, c_x, c_d, a_copy):
        cp.wait_send()


def attention(layer, x, lens, kc, vc, wq, wk, wv, wo, ids=None, n_local=0):
    tokens, d_model = x.shape
    rows, dim = kc.shape[2], kc.shape[3]
    heads = wq.shape[2] // dim
    half = tokens // 2
    hbm = pl.BlockSpec(memory_space=pltpu.HBM)
    vmem = pl.BlockSpec(memory_space=pltpu.VMEM)
    dma = pltpu.SemaphoreType.DMA
    scratch = [
        pltpu.VMEM((SLOTS, TB, rows, dim), BF16), pltpu.VMEM((SLOTS, TB, rows, dim), BF16), pltpu.VMEM((TB, heads, rows), BF16),
        pltpu.VMEM(wq.shape[1:], BF16), pltpu.VMEM(wk.shape[1:], BF16), pltpu.VMEM(wv.shape[1:], BF16), pltpu.VMEM(wo.shape[1:], BF16),
        pltpu.VMEM((tokens, heads, dim), F32), pltpu.VMEM((tokens, heads, dim), F32), pltpu.VMEM((half, heads, dim), F32),
        pltpu.VMEM((half, heads, dim), F32), pltpu.VMEM((half, heads, dim), F32),
        pltpu.VMEM((heads, 128), F32), pltpu.VMEM((heads, 128), F32), pltpu.VMEM((half, heads * dim), BF16),
        pltpu.VMEM((half, d_model), BF16),
        dma((SLOTS,)), dma((SLOTS,)), dma((4,)), dma((half // TB + 1,)), dma((half // TB + 1,)), dma((11,)), dma((11,)),
    ]
    out_shape = [jax.ShapeDtypeStruct((8, half, d_model), BF16)] + [jax.ShapeDtypeStruct((half, d_model // 2), BF16)] * 2
    in_specs = [vmem, pl.BlockSpec(memory_space=pltpu.SMEM)] + [hbm] * 6
    out_specs = [vmem] * 3
    args = [x, lens, kc, vc, wq, wk, wv, wo]
    if ids is not None:
        layers = ids.shape[0]
        args.append(ids)
        in_specs.append(vmem)
        out_shape += [jax.ShapeDtypeStruct((layers, 8, 8 * half), I32)] * 2 + [jax.ShapeDtypeStruct((layers, n_local, 128), I32)]
        out_specs += [vmem] * 3
        scratch += [pltpu.VMEM((4,) + ids.shape, I32), dma((3,)), dma((3,))]
    u, a, a_got, *rest = pl.pallas_call(
        functools.partial(attn_kernel, layer, ids is not None),
        out_shape=out_shape, in_specs=in_specs, out_specs=out_specs, scratch_shapes=scratch,
        compiler_params=pltpu.CompilerParams(collective_id=layer, has_side_effects=True, vmem_limit_bytes=VMEM_MIB[layer] << 20),
    )(*args)
    return (u.reshape(8 * half, d_model), a, a_got, *rest)


def expert_kernel(layer, part, off_ref, u_ref, pos_ref, w1_hbm, w3_hbm, w2_hbm, own_ref, send_ref,
                  xt, act, w1, w3, w2, t_exp, t_at, t_new, t_lo, t_hi, live, sem):
    n_tok = u_ref.shape[0]
    n_local = w1.shape[0]
    n_rows, cw = own_ref.shape
    p = lax.axis_index("pool")
    start = part * n_rows
    weights = ((w1_hbm, w1), (w3_hbm, w3), (w2_hbm, w2))

    def copies(e):
        return [pltpu.make_async_copy(src.at[layer, e], dst.at[e], sem.at[i, e]) for i, (src, dst) in enumerate(weights)]

    def plan(e, state):
        t, n = state
        end = jnp.where(e + 1 < n_local, off_ref[layer, jnp.minimum(e + 1, n_local - 1), 0], start + n_rows)
        lo = jnp.maximum(off_ref[layer, e, 0] - start, 0)
        hi = jnp.minimum(end - start, n_rows)
        base = lo // 16 * 16
        live[n] = e

        def put(i, t):
            t_exp[t] = e
            t_at[t] = jnp.minimum(base + i * TILE_M, n_rows - TILE_M)
            t_new[t] = jnp.where(i == 0, n + 1, 0)
            t_lo[t] = lo
            t_hi[t] = hi
            return t + 1

        some = lo < hi

        @pl.when(some & (n < DEPTH))
        def _():
            for cp in copies(e):
                cp.start()

        return lax.fori_loop(0, jnp.where(some, pl.cdiv(hi - base, TILE_M), 0), put, t), jnp.where(some, n + 1, n)

    tiles, n_live = lax.fori_loop(0, n_local, plan, (0, 0))
    t_new[tiles] = 0

    def start_nth(i):
        @pl.when(i < n_live)
        def _():
            for cp in copies(live[i]):
                cp.start()

    step = 128
    for r in range(n_rows // step):
        rid = lax.broadcasted_iota(I32, (step, n_tok), 0) + (r * step + start)
        hit = rid == pos_ref[layer, 0:1, :]
        for k in range(1, 6):
            hit = hit | (rid == pos_ref[layer, k:k + 1, :])
        rows = _nn(jnp.where(hit, 1.0, 0.0).astype(BF16), u_ref[...])
        xt[:, r * step:(r + 1) * step] = jnp.transpose(rows).astype(BF16)
    xt[:, n_rows:] = jnp.zeros((xt.shape[0], xt.shape[1] - n_rows), BF16)

    def arrive(k):
        @pl.when(t_new[k] > 0)
        def _():
            for cp in copies(t_exp[k]):
                cp.wait()
            start_nth(t_new[k] - 1 + DEPTH)

    def up(k):
        e, at = t_exp[k], t_at[k]
        cols = xt[:, pl.ds(pl.multiple_of(at // 128 * 128, 128), 2 * TILE_M)]
        h1 = _nn(w1[e], cols)
        h3 = _nn(w3[e], cols)
        return jnp.transpose(h1 * jax.nn.sigmoid(h1) * h3).astype(BF16)

    def down(k):
        at = pl.multiple_of(t_at[k], 16)
        rows = act[k % 2, pl.ds(pl.multiple_of(t_at[k] % 128, 16), TILE_M), :]
        rid = lax.broadcasted_iota(I32, (TILE_M, cw), 0) + at
        mask = (rid >= t_lo[k]) & (rid < t_hi[k])
        for ref, q in ((own_ref, p), (send_ref, 1 - p)):
            y = _nn(rows, w2[t_exp[k], :, pl.ds(pl.multiple_of(q * cw, 128), cw)])
            ref[pl.ds(at, TILE_M), :] = jnp.where(mask, y, ref[pl.ds(at, TILE_M), :])

    arrive(0)
    arrive(1)
    act[0] = up(0)

    def both(k, none):
        arrive(k + 1)
        act[k % 2] = up(k)
        down(k - 1)
        return none

    lax.fori_loop(1, tiles, both, 0)
    down(tiles - 1)


def experts(layer, part, off, u, pos_t, w1, w3, w2, n_rows):
    n_local, width, d_model = w1.shape[1:]
    hbm = pl.BlockSpec(memory_space=pl.ANY)
    vmem = pl.BlockSpec(memory_space=pltpu.VMEM)
    weights = pltpu.VMEM((n_local, width, d_model), BF16)
    table = pltpu.SMEM((64,), I32)
    return pl.pallas_call(
        functools.partial(expert_kernel, layer, part),
        out_shape=[jax.ShapeDtypeStruct((n_rows, d_model // 2), F32)] * 2,
        in_specs=[pl.BlockSpec(memory_space=pltpu.SMEM), vmem, vmem, hbm, hbm, hbm],
        out_specs=[vmem, vmem],
        scratch_shapes=[pltpu.VMEM((d_model, n_rows + 2 * TILE_M), BF16), pltpu.VMEM((2, 2 * TILE_M, width), BF16),
                        weights, weights, weights,
                        table, table, table, table, table, table, pltpu.SemaphoreType.DMA((3, n_local))],
        compiler_params=pltpu.CompilerParams(vmem_limit_bytes=45 << 20),
        cost_estimate=pl.CostEstimate(flops=int(4e9), bytes_accessed=18 << 20, transcendentals=0),
    )(off, u, pos_t, w1, w3, w2)


N_CH = 4


def combine_kernel(layer, *refs):
    early, refs = refs[:2 * (PARTS - 1)], refs[2 * (PARTS - 1):]
    _combine(layer, early, *refs)


def _combine(layer, early, own2_ref, send2_ref, u_ref, wr_ref, ids_ref, pos_ref, a_ref, a_got_ref, x_out,
                   yr, gm, tb, tcr, txs, txr, xo, a_buf, ysend, yrecv, csend, crecv, xsend, xrecv, fsend, frecv, lsem):
    p, _, x, c, to_y, to_x, to_c = _where_am_i()
    part_rows, cw = yr.shape[1], yr.shape[2]
    n_rows = PARTS * part_rows
    n_tok, top_k = u_ref.shape[0], 6
    tokens = 2 * a_ref.shape[0]
    mine = p * N_CH
    _greet((to_y, to_x, to_c))

    def cols(i):
        return pl.ds(pl.multiple_of(i * cw, 128), cw)

    y_copies = [_rcopy(send2_ref.at[:, j * cw:(j + 1) * cw], yr.at[j], ysend.at[j], yrecv.at[j], to_y) for j in range(N_CH)]
    for cp in y_copies:
        cp.start()

    half = a_ref.shape[0]
    a_buf[pl.ds(pl.multiple_of(p * half, half), half), :] = a_ref[...]
    a_buf[pl.ds(pl.multiple_of((1 - p) * half, half), half), :] = a_got_ref[...]
    step = 128
    n_exp = wr_ref.shape[1]
    wr = wr_ref[layer]
    wr1 = wr.astype(BF16)
    wr2 = (wr - wr1.astype(F32)).astype(BF16)
    wr3 = (wr - wr1.astype(F32) - wr2.astype(F32)).astype(BF16)

    def gates(i, carry):
        at = pl.ds(pl.multiple_of(i * step, step), step)
        rows = u_ref[at, :]
        logits = _nt(rows, wr1) + (_nt(rows, wr2) + _nt(rows, wr3))
        lane = lax.broadcasted_iota(I32, (step, n_exp), 1)
        ids = jnp.transpose(ids_ref[layer, :, at].astype(F32)).astype(I32)
        pos = jnp.transpose(pos_ref[layer, :, at].astype(F32)).astype(I32)
        g = [jnp.sum(jnp.where(lane == ids[:, k:k + 1], logits, 0.0), axis=1, keepdims=True) for k in range(top_k)]
        top = functools.reduce(jnp.maximum, g)
        g = [jnp.exp(v - top) for v in g]
        den = functools.reduce(jnp.add, g)
        g = [v / den for v in g]
        rid = lax.broadcasted_iota(I32, (step, n_rows), 1)
        mat = jnp.zeros((step, n_rows), F32)
        for k in range(top_k):
            mat = jnp.where(rid == pos[:, k:k + 1], g[k], mat)
        g1 = mat.astype(BF16)
        rest = mat - g1.astype(F32)
        g2 = rest.astype(BF16)
        gm[0, at, :] = g1
        gm[1, at, :] = g2
        gm[2, at, :] = (rest - g2.astype(F32)).astype(BF16)
        return carry

    lax.fori_loop(0, n_tok // step, gates, 0)

    def gated(ys, rows):
        return _nn(gm[0, :, rows], ys) + (_nn(gm[1, :, rows], ys) + _nn(gm[2, :, rows], ys))

    for j in range(N_CH):
        at = slice(j * cw, (j + 1) * cw)
        ys = [(early[2 * i][:, at] + early[2 * i + 1][:, at]).astype(BF16) for i in range(PARTS - 1)]
        tb[j] = gated(jnp.concatenate(ys, axis=0), pl.ds(0, n_rows - part_rows)).reshape(n_tok // tokens, tokens, cw)

    f_copies = []

    def finish(j, c_copies, x_copy):
        x_copy.wait_recv()
        own = tb[j, x * 2 + c] + tcr[j, x]
        new = (a_buf[:, j * cw:(j + 1) * cw].astype(F32) + (own + txr[j])).astype(BF16)
        xo[:, cols(mine + j)] = new
        f_copy = _rcopy(xo.at[:, cols(mine + j)], xo.at[:, cols(mine + j)], fsend.at[j], frecv.at[j], to_y)
        f_copy.start()
        f_copies.append((c_copies, x_copy, f_copy))

    last = None
    for j in range(N_CH):
        y_copies[j].wait_recv()
        ys = (own2_ref[:, j * cw:(j + 1) * cw] + yr[j]).astype(BF16)
        tb[j] = tb[j] + gated(ys, pl.ds(n_rows - part_rows, part_rows)).reshape(n_tok // tokens, tokens, cw)
        c_copies = [_rcopy(tb.at[j, i * 2 + (1 - c)], tcr.at[j, i], csend.at[j, i], crecv.at[j, i], to_c) for i in range(2)]
        for cp in c_copies:
            cp.start()
        if last is not None:
            finish(*last)
        for cp in c_copies:
            cp.wait_recv()
        txs[j] = tb[j, (1 - x) * 2 + c] + tcr[j, 1 - x]
        x_copy = _rcopy(txs.at[j], txr.at[j], xsend.at[j], xrecv.at[j], to_x)
        x_copy.start()
        last = (j, c_copies, x_copy)
    finish(*last)
    for _, _, f_copy in f_copies:
        f_copy.wait_recv()
    out = pltpu.make_async_copy(xo, x_out, lsem)
    out.start()
    for cp in y_copies:
        cp.wait_send()
    for c_copies, x_copy, f_copy in f_copies:
        for cp in c_copies:
            cp.wait_send()
        x_copy.wait_send()
        f_copy.wait_send()
    out.wait()


def combine(layer, early, own, send, u, wr, ids, pos, a, a_got):
    part_rows = own.shape[0]
    n_rows = PARTS * part_rows
    half, half_cols = a.shape
    tokens = 2 * half
    n_tok, d_model = u.shape
    cw = half_cols // N_CH
    vmem = pl.BlockSpec(memory_space=pltpu.VMEM)
    blocks = n_tok // tokens
    dma = pltpu.SemaphoreType.DMA
    return pl.pallas_call(
        functools.partial(combine_kernel, layer),
        out_shape=jax.ShapeDtypeStruct((tokens, d_model), BF16),
        in_specs=[vmem] * (len(early) + 8),
        out_specs=pl.BlockSpec(memory_space=pl.ANY),
        scratch_shapes=[
            pltpu.VMEM((N_CH, part_rows, cw), F32), pltpu.VMEM((3, n_tok, n_rows), BF16), pltpu.VMEM((N_CH, blocks, tokens, cw), F32),
            pltpu.VMEM((N_CH, 2, tokens, cw), F32), pltpu.VMEM((N_CH, tokens, cw), F32), pltpu.VMEM((N_CH, tokens, cw), F32),
            pltpu.VMEM((tokens, d_model), BF16), pltpu.VMEM((tokens, half_cols), BF16),
            dma((N_CH,)), dma((N_CH,)), dma((N_CH, 2)), dma((N_CH, 2)), dma((N_CH,)), dma((N_CH,)), dma((N_CH,)), dma((N_CH,)), dma,
        ],
        compiler_params=pltpu.CompilerParams(collective_id=2 + layer, has_side_effects=True, vmem_limit_bytes=32 << 20),
    )(*early, own, send, u, wr, ids, pos, a, a_got)


def solution(mesh):
    tok_spec = P(("dp", "ep"), None)
    cache_spec = P(None, ("dp", "ep"), "pool", None, None)
    up_spec = P(None, "ep", None, "pool")
    down_spec = P(None, "ep", "pool", None)
    in_specs = (tok_spec, cache_spec, cache_spec, P(("dp", "ep")), P(), P(), P(), P(), P(), P(None, ("dp", "ep"), None), up_spec, up_spec, down_spec)

    def body(hidden, kc, vc, lens, wq, wk, wv, wo, wr, ids, w1, w3, w2):
        layers, tokens, seq, heads, dim = kc.shape
        n_local = w1.shape[1]
        top_k = ids.shape[2]
        kc = kc.reshape(layers, tokens, seq * heads, dim)
        vc = vc.reshape(layers, tokens, seq * heads, dim)
        w1 = jnp.swapaxes(w1, 2, 3)
        w3 = jnp.swapaxes(w3, 2, 3)
        wr = jnp.swapaxes(wr, 1, 2)
        n_rows = tokens * top_k
        ids = jnp.pad(jnp.swapaxes(ids, 1, 2), ((0, 0), (0, 8 - top_k), (0, 0)))
        for layer in range(layers):
            first = layer == 0
            u, a, a_got, *tables = attention(layer, hidden, lens, kc, vc, wq, wk, wv, wo, ids if first else None, n_local)
            if first:
                pos, ids_all, off = tables
            early = []
            for part in range(PARTS):
                own, send = experts(layer, part, off, u, pos, w1, w3, w2, n_rows // PARTS)
                if part < PARTS - 1:
                    early += [own, lax.ppermute(send, "pool", [(0, 1), (1, 0)])]
            hidden = combine(layer, early, own, send, u, wr, ids_all, pos, a, a_got)
        return hidden

    return jax.shard_map(body, mesh=mesh, in_specs=in_specs, out_specs=tok_spec, check_vma=False)
```

profile of v0, /device:TPU:0, one launch (start us, length us, event | category | flops | bytes accessed | tf_op | source)
XLA Modules:
  0.0 177.8 jit_solution(8040070402906910403)
XLA Ops:
  0.0 0.7 copy.16
  0.7 0.0 copy-start.1
  0.7 0.9 copy-done.1
  1.7 0.0 copy-start.2
  1.7 0.7 copy-done.2
  2.3 28.6 %shard_map.127 = (bf16[8,64,1024]{2,1,0:T(8,128)(2,1)S(1)}, bf16[64,512]{1,0:T(8,128)(2,1)S(1)}, bf16[64,512]{1,0:T(8,128)(2,1)S(1)}, s32[2,8,512]{2,1,0:T(8,128...) custom-call(bf16[128,1024]{1,0:T(8,128)(2,1)S(1)} %copy-done.1, s32[128]{0:T(128)S(1)} %copy-done.2, ...), custom_call_target="tpu_custom_call" | custom-call | tf_op jit(solution)/shard_map/pallas_call | solution.py:297
  30.9 5.6 %shard_map.128 = (f32[256,512]{1,0:T(8,128)S(1)}, f32[256,512]{1,0:T(8,128)S(1)}) custom-call(s32[2,16,128]{2,1,0:T(8,128)S(1)} %get-tuple-element.26.off_ref, bf16[512,1024]{1,0:T(8,128)(2,1)S(1)} %bitcast.10, s32[2,8,512]{2,1,0:T(8,128)S(1)} %get-tuple-element.28.pos_ref.refs_9_, bf16[2,16,352,1024]{3,2,1,0:T(8,128)(2,1)} %bitcast.20, ...), custom_call_target="tpu_custom_call" | custom-call | flops 4000000000 | bytes 18874368 | tf_op jit(solution)/shard_map/pallas_call | solution.py:404
  36.5 0.4 collective-permute-start
  36.9 7.2 %shard_map.129 = (f32[256,512]{1,0:T(8,128)S(1)}, f32[256,512]{1,0:T(8,128)S(1)}) custom-call(s32[2,16,128]{2,1,0:T(8,128)S(1)} %get-tuple-element.26.off_ref, bf16[512,1024]{1,0:T(8,128)(2,1)S(1)} %bitcast.11, s32[2,8,512]{2,1,0:T(8,128)S(1)} %get-tuple-element.28.pos_ref.refs_9_, bf16[2,16,352,1024]{3,2,1,0:T(8,128)(2,1)} %bitcast.21, ...), custom_call_target="tpu_custom_call" | custom-call | flops 4000000000 | bytes 18874368 | tf_op jit(solution)/shard_map/pallas_call | solution.py:404
  44.1 0.0 copy-start
  44.1 0.0 copy-start.3
  44.1 1.7 collective-permute-start.1
  45.8 14.9 %shard_map.130 = (f32[256,512]{1,0:T(8,128)S(1)}, f32[256,512]{1,0:T(8,128)S(1)}) custom-call(s32[2,16,128]{2,1,0:T(8,128)S(1)} %get-tuple-element.26.off_ref, bf16[512,1024]{1,0:T(8,128)(2,1)S(1)} %bitcast.12, s32[2,8,512]{2,1,0:T(8,128)S(1)} %get-tuple-element.28.pos_ref.refs_9_, bf16[2,16,352,1024]{3,2,1,0:T(8,128)(2,1)} %bitcast.22, ...), custom_call_target="tpu_custom_call" | custom-call | flops 4000000000 | bytes 18874368 | tf_op jit(solution)/shard_map/pallas_call | solution.py:404
  60.7 0.0 collective-permute-done.refs_1_
  60.8 1.2 collective-permute-done.1.refs_3_
  62.0 0.0 copy-done
  62.0 25.2 %shard_map.131.x_ref = bf16[128,1024]{1,0:T(8,128)(2,1)S(1)} custom-call(f32[256,512]{1,0:T(8,128)S(1)} %get-tuple-element.29.refs_0_, f32[256,512]{1,0:T(8,128)S(1)} %collective-permute-done.refs_1_, f32[256,512]{1,0:T(8,128)S(1)} %get-tuple-element.31.refs_2_, f32[256,512]{1,0:T(8,128)S(1)} %collective-permute-done.1.refs_3_, ...), custom_call_target="tpu_custom_call" | custom-call | tf_op jit(solution)/shard_map/pallas_call | solution.py:538
  87.2 0.0 copy-done.3
  87.2 24.9 %shard_map.132 = (bf16[8,64,1024]{2,1,0:T(8,128)(2,1)S(1)}, bf16[64,512]{1,0:T(8,128)(2,1)S(1)}, bf16[64,512]{1,0:T(8,128)(2,1)S(1)}) custom-call(bf16[128,1024]{1,0:T(8,128)(2,1)S(1)} %shard_map.131.x_ref, s32[128]{0:T(128)S(1)} %copy-done.3, bf16[2,128,512,128]{3,2,1,0:T(8,128)(2,1)} %bitcast.33, bf16[2,128,512,128]{3,2,1,0:T(8,128)(2,1)} %bitcast.35, ...), custom_call_target="tpu_custom_call" | custom-call | tf_op jit(solution)/shard_map/pallas_call | solution.py:297
  112.1 5.6 %shard_map.133 = (f32[256,512]{1,0:T(8,128)S(1)}, f32[256,512]{1,0:T(8,128)S(1)}) custom-call(s32[2,16,128]{2,1,0:T(8,128)S(1)} %get-tuple-element.26.off_ref, bf16[512,1024]{1,0:T(8,128)(2,1)S(1)} %bitcast.14, s32[2,8,512]{2,1,0:T(8,128)S(1)} %get-tuple-element.28.pos_ref.refs_9_, bf16[2,16,352,1024]{3,2,1,0:T(8,128)(2,1)} %bitcast.23, ...), custom_call_target="tpu_custom_call" | custom-call | flops 4000000000 | bytes 18874368 | tf_op jit(solution)/shard_map/pallas_call | solution.py:404
  117.7 8.4 %shard_map.134 = (f32[256,512]{1,0:T(8,128)S(1)}, f32[256,512]{1,0:T(8,128)S(1)}) custom-call(s32[2,16,128]{2,1,0:T(8,128)S(1)} %get-tuple-element.26.off_ref, bf16[512,1024]{1,0:T(8,128)(2,1)S(1)} %bitcast.15, s32[2,8,512]{2,1,0:T(8,128)S(1)} %get-tuple-element.28.pos_ref.refs_9_, bf16[2,16,352,1024]{3,2,1,0:T(8,128)(2,1)} %bitcast.24, ...), custom_call_target="tpu_custom_call" | custom-call | flops 4000000000 | bytes 18874368 | tf_op jit(solution)/shard_map/pallas_call | solution.py:404
  126.1 1.2 collective-permute-start.2
  127.3 0.8 collective-permute-start.3
  128.2 13.9 %shard_map.135 = (f32[256,512]{1,0:T(8,128)S(1)}, f32[256,512]{1,0:T(8,128)S(1)}) custom-call(s32[2,16,128]{2,1,0:T(8,128)S(1)} %get-tuple-element.26.off_ref, bf16[512,1024]{1,0:T(8,128)(2,1)S(1)} %bitcast.16, s32[2,8,512]{2,1,0:T(8,128)S(1)} %get-tuple-element.28.pos_ref.refs_9_, bf16[2,16,352,1024]{3,2,1,0:T(8,128)(2,1)} %bitcast.25, ...), custom_call_target="tpu_custom_call" | custom-call | flops 4000000000 | bytes 18874368 | tf_op jit(solution)/shard_map/pallas_call | solution.py:404
  142.1 0.0 collective-permute-done.2.refs_1_
  142.1 9.5 %collective-permute-done.3.refs_3_ = f32[256,512]{1,0:T(8,128)S(1)} collective-permute-done((f32[256,512]{1,0:T(8,128)S(1)}, f32[256,512]{1,0:T(8,128)S(1)}, u32[]{:S(2)}, u32[]{:S(2)}) %collective-permute-start.3) | collective-permute-done | bytes 524320 | tf_op jit(solution)/shard_map/ppermute | solution.py:580
  151.6 25.5 %shard_map.136 = bf16[128,1024]{1,0:T(8,128)(2,1)S(1)} custom-call(f32[256,512]{1,0:T(8,128)S(1)} %get-tuple-element.39.refs_0_, f32[256,512]{1,0:T(8,128)S(1)} %collective-permute-done.2.refs_1_, f32[256,512]{1,0:T(8,128)S(1)} %get-tuple-element.41.refs_2_, f32[256,512]{1,0:T(8,128)S(1)} %collective-permute-done.3.refs_3_, ...), custom_call_target="tpu_custom_call" | custom-call | tf_op jit(solution)/shard_map/pallas_call | solution.py:538
  177.1 0.7 copy.18
  (1 shorter events, 0.0 us)
Async XLA Ops:
  0.7 0.9 copy-start.1
  1.7 0.7 copy-start.2
  36.5 24.3 %collective-permute-start = (f32[256,512]{1,0:T(8,128)S(1)}, f32[256,512]{1,0:T(8,128)S(1)}, u32[]{:S(2)}, u32[]{:S(2)}) collective-permute-start(f32[256,512]{1,0:T(8,128)S(1)} %get-tuple-element.30), channel_id=1, source_target_pairs={{0,4},{4,0},{1,5},{5,1},{2,6},{6,2},{3,7},{7,3}} | collective-permute-start | bytes 1572872 | tf_op jit(solution)/shard_map/ppermute | solution.py:580
  44.1 17.9 %copy-start = (f32[2,1024,64]{1,2,0:T(8,128)S(1)}, f32[2,1024,64]{1,2,0:T(8,128)}, u32[]{:S(2)}) copy-start(f32[2,1024,64]{1,2,0:T(8,128)} %param.21) | copy-start | bytes 1572868
  44.1 43.1 %copy-start.3 = (s32[128]{0:T(128)S(1)}, s32[128]{0:T(128)}, u32[]{:S(2)}) copy-start(s32[128]{0:T(128)} %len_ref.3) | copy-start | bytes 1540
  44.1 17.8 %collective-permute-start.1 = (f32[256,512]{1,0:T(8,128)S(1)}, f32[256,512]{1,0:T(8,128)S(1)}, u32[]{:S(2)}, u32[]{:S(2)}) collective-permute-start(f32[256,512]{1,0:T(8,128)S(1)} %get-tuple-element.32), channel_id=1, source_target_pairs={{0,4},{4,0},{1,5},{5,1},{2,6},{6,2},{3,7},{7,3}} | collective-permute-start | bytes 1572872 | tf_op jit(solution)/shard_map/ppermute | solution.py:580
  126.1 15.9 %collective-permute-start.2 = (f32[256,512]{1,0:T(8,128)S(1)}, f32[256,512]{1,0:T(8,128)S(1)}, u32[]{:S(2)}, u32[]{:S(2)}) collective-permute-start(f32[256,512]{1,0:T(8,128)S(1)} %get-tuple-element.40), channel_id=1, source_target_pairs={{0,4},{4,0},{1,5},{5,1},{2,6},{6,2},{3,7},{7,3}} | collective-permute-start | bytes 1572872 | tf_op jit(solution)/shard_map/ppermute | solution.py:580
  127.3 24.3 %collective-permute-start.3 = (f32[256,512]{1,0:T(8,128)S(1)}, f32[256,512]{1,0:T(8,128)S(1)}, u32[]{:S(2)}, u32[]{:S(2)}) collective-permute-start(f32[256,512]{1,0:T(8,128)S(1)} %get-tuple-element.42), channel_id=1, source_target_pairs={{0,4},{4,0},{1,5},{5,1},{2,6},{6,2},{3,7},{7,3}} | collective-permute-start | bytes 1572872 | tf_op jit(solution)/shard_map/ppermute | solution.py:580
where the time goes:
time: 178 us
  Pallas kernels  160 us (90%)
  waiting for transfers between devices  10.7 us (6%)
  starting transfers between devices  4.11 us (2%)
  local copies, waits for them, and re-layouts  3.02 us (2%)
    pallas_call x6, Pallas kernels, experts(): pl.pallas_call(functools.partial(expert_kernel, layer, part), out_shape=[...  55.6 us
    pallas_call x2, Pallas kernels, attention(): pl.pallas_call(functools.partial(attn_kernel, layer, ids is not None), ou...  53.5 us
    pallas_call x2, Pallas kernels, combine(): pl.pallas_call(functools.partial(combine_kernel, layer), out_shape=jax.Sh...  50.7 us
    ppermute x4, waiting for transfers between devices, body(): early += [own, lax.ppermute(send, 'pool', [(0, 1), (1, 0)])]  10.7 us
    ppermute x4, starting transfers between devices, body(): early += [own, lax.ppermute(send, 'pool', [(0, 1), (1, 0)])]  4.11 us
  transfers between devices with their start and end apart: 4, of which 2 were waited for; matrix products, arithmetic and copies ran while one was open for 0% of the time, Pallas kernels for 20%

commit v1 on v0

--- a/solution.py
+++ b/solution.py
@@ -17,7 +17,8 @@
 TB = 8
 SLOTS = 4
 TILE_M = 128
-PARTS = 3
+PART_ROWS = (256, 384, 128)
+PARTS = len(PART_ROWS)
 DEPTH = 4
 VMEM_MIB = (51, 51)
 
@@ -308,7 +309,7 @@
     n_local = w1.shape[0]
     n_rows, cw = own_ref.shape
     p = lax.axis_index("pool")
-    start = part * n_rows
+    start = sum(PART_ROWS[:part])
     weights = ((w1_hbm, w1), (w3_hbm, w3), (w2_hbm, w2))
 
     def copies(e):
@@ -417,31 +418,12 @@
 N_CH = 4
 
 
-def combine_kernel(layer, *refs):
-    early, refs = refs[:2 * (PARTS - 1)], refs[2 * (PARTS - 1):]
-    _combine(layer, early, *refs)
-
-
-def _combine(layer, early, own2_ref, send2_ref, u_ref, wr_ref, ids_ref, pos_ref, a_ref, a_got_ref, x_out,
-                   yr, gm, tb, tcr, txs, txr, xo, a_buf, ysend, yrecv, csend, crecv, xsend, xrecv, fsend, frecv, lsem):
-    p, _, x, c, to_y, to_x, to_c = _where_am_i()
-    part_rows, cw = yr.shape[1], yr.shape[2]
-    n_rows = PARTS * part_rows
-    n_tok, top_k = u_ref.shape[0], 6
-    tokens = 2 * a_ref.shape[0]
-    mine = p * N_CH
-    _greet((to_y, to_x, to_c))
-
-    def cols(i):
-        return pl.ds(pl.multiple_of(i * cw, 128), cw)
-
-    y_copies = [_rcopy(send2_ref.at[:, j * cw:(j + 1) * cw], yr.at[j], ysend.at[j], yrecv.at[j], to_y) for j in range(N_CH)]
-    for cp in y_copies:
-        cp.start()
-
-    half = a_ref.shape[0]
-    a_buf[pl.ds(pl.multiple_of(p * half, half), half), :] = a_ref[...]
-    a_buf[pl.ds(pl.multiple_of((1 - p) * half, half), half), :] = a_got_ref[...]
+def _gated(gm, rows, ys):
+    return _nn(gm[0, :, rows], ys) + (_nn(gm[1, :, rows], ys) + _nn(gm[2, :, rows], ys))
+
+
+def gate_kernel(layer, own_ref, got_ref, u_ref, wr_ref, ids_ref, pos_ref, gm, t0):
+    n_rows, n_tok, top_k = gm.shape[2], gm.shape[1], 6
     step = 128
     n_exp = wr_ref.shape[1]
     wr = wr_ref[layer]
@@ -475,79 +457,115 @@
 
     lax.fori_loop(0, n_tok // step, gates, 0)
 
-    def gated(ys, rows):
-        return _nn(gm[0, :, rows], ys) + (_nn(gm[1, :, rows], ys) + _nn(gm[2, :, rows], ys))
-
+    part_rows, cols = own_ref.shape
+    total = _gated(gm, pl.ds(0, part_rows), (own_ref[...] + got_ref[...]).astype(BF16))
+    cw = cols // N_CH
     for j in range(N_CH):
-        at = slice(j * cw, (j + 1) * cw)
-        ys = [(early[2 * i][:, at] + early[2 * i + 1][:, at]).astype(BF16) for i in range(PARTS - 1)]
-        tb[j] = gated(jnp.concatenate(ys, axis=0), pl.ds(0, n_rows - part_rows)).reshape(n_tok // tokens, tokens, cw)
-
-    f_copies = []
-
-    def finish(j, c_copies, x_copy):
-        x_copy.wait_recv()
+        t0[j] = total[:, j * cw:(j + 1) * cw].reshape(t0.shape[1:])
+
+
+def gates(layer, own, got, u, wr, ids, pos):
+    n_tok = u.shape[0]
+    tokens = n_tok // 4
+    vmem = pl.BlockSpec(memory_space=pltpu.VMEM)
+    return pl.pallas_call(
+        functools.partial(gate_kernel, layer),
+        out_shape=[jax.ShapeDtypeStruct((3, n_tok, sum(PART_ROWS)), BF16),
+                   jax.ShapeDtypeStruct((N_CH, 4, tokens, own.shape[1] // N_CH), F32)],
+        in_specs=[vmem] * 6, out_specs=[vmem] * 2,
+        compiler_params=pltpu.CompilerParams(vmem_limit_bytes=20 << 20),
+        cost_estimate=pl.CostEstimate(flops=int(2e9), bytes_accessed=4 << 20, transcendentals=0),
+    )(own, got, u, wr, ids, pos)
+
+
+def combine_kernel(own1_ref, got1_ref, own2_ref, send2_ref, gm, t0_ref, a_ref, a_got_ref, x_out,
+                   yr, tb, tcr, txs, txr, xo, a_buf, ysend, yrecv, csend, crecv, xsend, xrecv, fsend, frecv, lsem):
+    p, _, x, c, to_y, to_x, to_c = _where_am_i()
+    cw = yr.shape[2]
+    mine = p * N_CH
+    _greet((to_y, to_x, to_c))
+
+    def cols(i):
+        return pl.ds(pl.multiple_of(i * cw, 128), cw)
+
+    y_copies = [_rcopy(send2_ref.at[:, j * cw:(j + 1) * cw], yr.at[j], ysend.at[j], yrecv.at[j], to_y) for j in range(N_CH)]
+    for cp in y_copies:
+        cp.start()
+
+    half = a_ref.shape[0]
+    a_buf[pl.ds(pl.multiple_of(p * half, half), half), :] = a_ref[...]
+    a_buf[pl.ds(pl.multiple_of((1 - p) * half, half), half), :] = a_got_ref[...]
+    second, third = pl.ds(PART_ROWS[0], PART_ROWS[1]), pl.ds(PART_ROWS[0] + PART_ROWS[1], PART_ROWS[2])
+    total = _gated(gm, second, (own1_ref[...] + got1_ref[...]).astype(BF16))
+    for j in range(N_CH):
+        tb[j] = t0_ref[j] + total[:, j * cw:(j + 1) * cw].reshape(tb.shape[1:])
+
+    chunks = []
+
+    def gather(j):
+        y_copies[j].wait_recv()
+        ys = (own2_ref[:, j * cw:(j + 1) * cw] + yr[j]).astype(BF16)
+        tb[j] = tb[j] + _gated(gm, third, ys).reshape(tb.shape[1:])
+        c_copies = [_rcopy(tb.at[j, i * 2 + (1 - c)], tcr.at[j, i], csend.at[j, i], crecv.at[j, i], to_c) for i in range(2)]
+        for cp in c_copies:
+            cp.start()
+        chunks.append(c_copies)
+
+    def cross(j):
+        for cp in chunks[j]:
+            cp.wait_recv()
+        txs[j] = tb[j, (1 - x) * 2 + c] + tcr[j, 1 - x]
+        x_copy = _rcopy(txs.at[j], txr.at[j], xsend.at[j], xrecv.at[j], to_x)
+        x_copy.start()
+        chunks[j].append(x_copy)
+
+    def finish(j):
+        chunks[j][-1].wait_recv()
         own = tb[j, x * 2 + c] + tcr[j, x]
         new = (a_buf[:, j * cw:(j + 1) * cw].astype(F32) + (own + txr[j])).astype(BF16)
         xo[:, cols(mine + j)] = new
         f_copy = _rcopy(xo.at[:, cols(mine + j)], xo.at[:, cols(mine + j)], fsend.at[j], frecv.at[j], to_y)
         f_copy.start()
-        f_copies.append((c_copies, x_copy, f_copy))
-
-    last = None
-    for j in range(N_CH):
-        y_copies[j].wait_recv()
-        ys = (own2_ref[:, j * cw:(j + 1) * cw] + yr[j]).astype(BF16)
-        tb[j] = tb[j] + gated(ys, pl.ds(n_rows - part_rows, part_rows)).reshape(n_tok // tokens, tokens, cw)
-        c_copies = [_rcopy(tb.at[j, i * 2 + (1 - c)], tcr.at[j, i], csend.at[j, i], crecv.at[j, i], to_c) for i in range(2)]
-        for cp in c_copies:
-            cp.start()
-        if last is not None:
-            finish(*last)
-        for cp in c_copies:
-            cp.wait_recv()
-        txs[j] = tb[j, (1 - x) * 2 + c] + tcr[j, 1 - x]
-        x_copy = _rcopy(txs.at[j], txr.at[j], xsend.at[j], xrecv.at[j], to_x)
-        x_copy.start()
-        last = (j, c_copies, x_copy)
-    finish(*last)
-    for _, _, f_copy in f_copies:
-        f_copy.wait_recv()
+        chunks[j].append(f_copy)
+
+    for j in range(N_CH + 2):
+        if j < N_CH:
+            gather(j)
+        if 0 <= j - 1 < N_CH:
+            cross(j - 1)
+        if 0 <= j - 2 < N_CH:
+            finish(j - 2)
+    for copies in chunks:
+        copies[-1].wait_recv()
     out = pltpu.make_async_copy(xo, x_out, lsem)
     out.start()
     for cp in y_copies:
         cp.wait_send()
-    for c_copies, x_copy, f_copy in f_copies:
-        for cp in c_copies:
+    for copies in chunks:
+        for cp in copies:
             cp.wait_send()
-        x_copy.wait_send()
-        f_copy.wait_send()
     out.wait()
 
 
-def combine(layer, early, own, send, u, wr, ids, pos, a, a_got):
-    part_rows = own.shape[0]
-    n_rows = PARTS * part_rows
+def combine(layer, own1, got1, own2, send2, gm, t0, a, a_got):
     half, half_cols = a.shape
     tokens = 2 * half
-    n_tok, d_model = u.shape
     cw = half_cols // N_CH
     vmem = pl.BlockSpec(memory_space=pltpu.VMEM)
-    blocks = n_tok // tokens
     dma = pltpu.SemaphoreType.DMA
     return pl.pallas_call(
-        functools.partial(combine_kernel, layer),
-        out_shape=jax.ShapeDtypeStruct((tokens, d_model), BF16),
-        in_specs=[vmem] * (len(early) + 8),
+        combine_kernel,
+        out_shape=jax.ShapeDtypeStruct((tokens, 2 * half_cols), BF16),
+        in_specs=[vmem] * 8,
         out_specs=pl.BlockSpec(memory_space=pl.ANY),
         scratch_shapes=[
-            pltpu.VMEM((N_CH, part_rows, cw), F32), pltpu.VMEM((3, n_tok, n_rows), BF16), pltpu.VMEM((N_CH, blocks, tokens, cw), F32),
+            pltpu.VMEM((N_CH, own2.shape[0], cw), F32), pltpu.VMEM(t0.shape, F32),
             pltpu.VMEM((N_CH, 2, tokens, cw), F32), pltpu.VMEM((N_CH, tokens, cw), F32), pltpu.VMEM((N_CH, tokens, cw), F32),
-            pltpu.VMEM((tokens, d_model), BF16), pltpu.VMEM((tokens, half_cols), BF16),
+            pltpu.VMEM((tokens, 2 * half_cols), BF16), pltpu.VMEM((tokens, half_cols), BF16),
             dma((N_CH,)), dma((N_CH,)), dma((N_CH, 2)), dma((N_CH, 2)), dma((N_CH,)), dma((N_CH,)), dma((N_CH,)), dma((N_CH,)), dma,
         ],
         compiler_params=pltpu.CompilerParams(collective_id=2 + layer, has_side_effects=True, vmem_limit_bytes=32 << 20),
-    )(*early, own, send, u, wr, ids, pos, a, a_got)
+    )(own1, got1, own2, send2, gm, t0, a, a_got)
 
 
 def solution(mesh):
@@ -566,19 +584,20 @@
         w1 = jnp.swapaxes(w1, 2, 3)
         w3 = jnp.swapaxes(w3, 2, 3)
         wr = jnp.swapaxes(wr, 1, 2)
-        n_rows = tokens * top_k
         ids = jnp.pad(jnp.swapaxes(ids, 1, 2), ((0, 0), (0, 8 - top_k), (0, 0)))
         for layer in range(layers):
             first = layer == 0
             u, a, a_got, *tables = attention(layer, hidden, lens, kc, vc, wq, wk, wv, wo, ids if first else None, n_local)
             if first:
                 pos, ids_all, off = tables
-            early = []
+            own, got = [], []
             for part in range(PARTS):
-                own, send = experts(layer, part, off, u, pos, w1, w3, w2, n_rows // PARTS)
+                kept, send = experts(layer, part, off, u, pos, w1, w3, w2, PART_ROWS[part])
+                own.append(kept)
                 if part < PARTS - 1:
-                    early += [own, lax.ppermute(send, "pool", [(0, 1), (1, 0)])]
-            hidden = combine(layer, early, own, send, u, wr, ids_all, pos, a, a_got)
+                    got.append(lax.ppermute(send, "pool", [(0, 1), (1, 0)]))
+            gm, t0 = gates(layer, own[0], got[0], u, wr, ids_all, pos)
+            hidden = combine(layer, own[1], got[1], own[2], send, gm, t0, a, a_got)
         return hidden
 
     return jax.shard_map(body, mesh=mesh, in_specs=in_specs, out_specs=tok_spec, check_vma=False)

time: 178 us -> 186 us (1.045)
  waiting for transfers between devices: 10.7 us -> 21.6 us
  Pallas kernels: 160 us -> 157 us
    ppermute x4, waiting for transfers between devices: 10.7 us -> 21.6 us  [body(): got.append(lax.ppermute(send, 'pool', [(0, 1), (1, 0)]))]
    pallas_call x2 -> x4, Pallas kernels: 50.7 us -> 47.8 us  [the longest x2 37.9 us: combine(): pl.pallas_call(combine_kernel, out_shape=jax.ShapeDtypeStruct((tokens, 2...]
  transfers between devices with their start and end apart: 4 -> 4, of which waited for: 2 -> 2; matrix products, arithmetic and copies ran while one was open for 0% -> 0% of each run, Pallas kernels for 20% -> 25%
where the time goes in v1:
time: 186 us
  Pallas kernels  157 us (84%)
  waiting for transfers between devices  21.6 us (12%)
  starting transfers between devices  4.13 us (2%)
  local copies, waits for them, and re-layouts  3.02 us (2%)
    pallas_call x6, Pallas kernels, experts(): pl.pallas_call(functools.partial(expert_kernel, layer, part), out_shape=[...  55.8 us
    pallas_call x2, Pallas kernels, attention(): pl.pallas_call(functools.partial(attn_kernel, layer, ids is not None), ou...  53.2 us
    pallas_call x2, Pallas kernels, combine(): pl.pallas_call(combine_kernel, out_shape=jax.ShapeDtypeStruct((tokens, 2...  37.9 us
    ppermute x4, waiting for transfers between devices, body(): got.append(lax.ppermute(send, 'pool', [(0, 1), (1, 0)]))  21.6 us
    pallas_call x2, Pallas kernels, gates(): pl.pallas_call(functools.partial(gate_kernel, layer), out_shape=[jax.Shap...  9.92 us
    ppermute x4, starting transfers between devices, body(): got.append(lax.ppermute(send, 'pool', [(0, 1), (1, 0)]))  4.13 us
  transfers between devices with their start and end apart: 4, of which 2 were waited for; matrix products, arithmetic and copies ran while one was open for 0% of the time, Pallas kernels for 25%

profile of v1, /device:TPU:0, one launch (start us, length us, event | category | flops | bytes accessed | tf_op | source)
XLA Modules:
  0.0 185.7 jit_solution(5268829486732417367)
XLA Ops:
  0.0 0.7 copy.16
  0.7 0.0 copy-start
  0.7 0.9 copy-done
  1.7 0.0 copy-start.1
  1.7 0.7 copy-done.1
  2.3 28.6 %shard_map.127 = (bf16[8,64,1024]{2,1,0:T(8,128)(2,1)S(1)}, bf16[64,512]{1,0:T(8,128)(2,1)S(1)}, bf16[64,512]{1,0:T(8,128)(2,1)S(1)}, s32[2,8,512]{2,1,0:T(8,128...) custom-call(bf16[128,1024]{1,0:T(8,128)(2,1)S(1)} %copy-done, s32[128]{0:T(128)S(1)} %copy-done.1, ...), custom_call_target="tpu_custom_call" | custom-call | tf_op jit(solution)/shard_map/pallas_call | solution.py:298
  30.9 10.0 %shard_map.128 = (f32[384,512]{1,0:T(8,128)S(1)}, f32[384,512]{1,0:T(8,128)S(1)}) custom-call(s32[2,16,128]{2,1,0:T(8,128)S(1)} %get-tuple-element.30.off_ref, bf16[512,1024]{1,0:T(8,128)(2,1)S(1)} %bitcast.10, s32[2,8,512]{2,1,0:T(8,128)S(1)} %get-tuple-element.32.pos_ref, bf16[2,16,352,1024]{3,2,1,0:T(8,128)(2,1)} %bitcast.20, ...), custom_call_target="tpu_custom_call" | custom-call | flops 4000000000 | bytes 18874368 | tf_op jit(solution)/shard_map/pallas_call | solution.py:405
  40.9 0.4 collective-permute-start
  41.3 5.6 %shard_map.130 = (f32[256,512]{1,0:T(8,128)S(1)}, f32[256,512]{1,0:T(8,128)S(1)}) custom-call(s32[2,16,128]{2,1,0:T(8,128)S(1)} %get-tuple-element.30.off_ref, bf16[512,1024]{1,0:T(8,128)(2,1)S(1)} %bitcast.11, s32[2,8,512]{2,1,0:T(8,128)S(1)} %get-tuple-element.32.pos_ref, bf16[2,16,352,1024]{3,2,1,0:T(8,128)(2,1)} %bitcast.21, ...), custom_call_target="tpu_custom_call" | custom-call | flops 4000000000 | bytes 18874368 | tf_op jit(solution)/shard_map/pallas_call | solution.py:405
  46.9 0.0 copy-start.3
  46.9 1.7 collective-permute-start.1
  48.6 12.2 %shard_map.129 = (f32[128,512]{1,0:T(8,128)S(1)}, f32[128,512]{1,0:T(8,128)S(1)}) custom-call(s32[2,16,128]{2,1,0:T(8,128)S(1)} %get-tuple-element.30.off_ref, bf16[512,1024]{1,0:T(8,128)(2,1)S(1)} %bitcast.12, s32[2,8,512]{2,1,0:T(8,128)S(1)} %get-tuple-element.32.pos_ref, bf16[2,16,352,1024]{3,2,1,0:T(8,128)(2,1)} %bitcast.22, ...), custom_call_target="tpu_custom_call" | custom-call | flops 4000000000 | bytes 18874368 | tf_op jit(solution)/shard_map/pallas_call | solution.py:405
  60.8 10.3 %collective-permute-done.1.got_ref = f32[256,512]{1,0:T(8,128)S(1)} collective-permute-done((f32[256,512]{1,0:T(8,128)S(1)}, f32[256,512]{1,0:T(8,128)S(1)}, u32[]{:S(2)}, u32[]{:S(2)}) %collective-permute-start.1) | collective-permute-done | bytes 524320 | tf_op jit(solution)/shard_map/ppermute | solution.py:598
  71.1 0.0 copy-done.3
  71.1 5.0 %shard_map.131 = (bf16[3,512,768]{2,1,0:T(8,128)(2,1)S(1)}, f32[4,4,128,128]{3,2,1,0:T(8,128)S(1)}) custom-call(f32[256,512]{1,0:T(8,128)S(1)} %get-tuple-element.37.own_ref, f32[256,512]{1,0:T(8,128)S(1)} %collective-permute-done.1.got_ref, bf16[512,1024]{1,0:T(8,128)(2,1)S(1)} %bitcast.13, f32[2,64,1024]{2,1,0:T(8,128)S(1)} %bitcast.18, ...), custom_call_target="tpu_custom_call" | custom-call | flops 2000000000 | bytes 4194304 | tf_op jit(solution)/shard_map/pallas_call | solution.py:471
  76.0 0.0 copy-start.2
  76.0 0.0 collective-permute-done.got1_ref
  76.1 18.8 %shard_map.132.x_ref = bf16[128,1024]{1,0:T(8,128)(2,1)S(1)} custom-call(f32[384,512]{1,0:T(8,128)S(1)} %get-tuple-element.33.own1_ref, f32[384,512]{1,0:T(8,128)S(1)} %collective-permute-done.got1_ref, f32[128,512]{1,0:T(8,128)S(1)} %get-tuple-element.35.own2_ref, f32[128,512]{1,0:T(8,128)S(1)} %get-tuple-element.36.send2_ref, ...), custom_call_target="tpu_custom_call" | custom-call | tf_op jit(solution)/shard_map/pallas_call | solution.py:556
  94.8 0.0 copy-done.2
  94.8 24.7 %shard_map.133 = (bf16[8,64,1024]{2,1,0:T(8,128)(2,1)S(1)}, bf16[64,512]{1,0:T(8,128)(2,1)S(1)}, bf16[64,512]{1,0:T(8,128)(2,1)S(1)}) custom-call(bf16[128,1024]{1,0:T(8,128)(2,1)S(1)} %shard_map.132.x_ref, s32[128]{0:T(128)S(1)} %copy-done.2, bf16[2,128,512,128]{3,2,1,0:T(8,128)(2,1)} %bitcast.33, bf16[2,128,512,128]{3,2,1,0:T(8,128)(2,1)} %bitcast.35, ...), custom_call_target="tpu_custom_call" | custom-call | tf_op jit(solution)/shard_map/pallas_call | solution.py:298
  119.5 10.0 %shard_map.134 = (f32[384,512]{1,0:T(8,128)S(1)}, f32[384,512]{1,0:T(8,128)S(1)}) custom-call(s32[2,16,128]{2,1,0:T(8,128)S(1)} %get-tuple-element.30.off_ref, bf16[512,1024]{1,0:T(8,128)(2,1)S(1)} %bitcast.14, s32[2,8,512]{2,1,0:T(8,128)S(1)} %get-tuple-element.32.pos_ref, bf16[2,16,352,1024]{3,2,1,0:T(8,128)(2,1)} %bitcast.23, ...), custom_call_target="tpu_custom_call" | custom-call | flops 4000000000 | bytes 18874368 | tf_op jit(solution)/shard_map/pallas_call | solution.py:405
  129.6 2.0 %collective-permute-start.2 = (f32[384,512]{1,0:T(8,128)S(1)}, f32[384,512]{1,0:T(8,128)S(1)}, u32[]{:S(2)}, u32[]{:S(2)}) collective-permute-start(f32[384,512]{1,0:T(8,128)S(1)} %get-tuple-element.46), channel_id=1, source_target_pairs={{0,4},{4,0},{1,5},{5,1},{2,6},{6,2},{3,7},{7,3}} | collective-permute-start | bytes 2359304 | tf_op jit(solution)/shard_map/ppermute | solution.py:598
  131.6 5.6 %shard_map.136 = (f32[256,512]{1,0:T(8,128)S(1)}, f32[256,512]{1,0:T(8,128)S(1)}) custom-call(s32[2,16,128]{2,1,0:T(8,128)S(1)} %get-tuple-element.30.off_ref, bf16[512,1024]{1,0:T(8,128)(2,1)S(1)} %bitcast.15, s32[2,8,512]{2,1,0:T(8,128)S(1)} %get-tuple-element.32.pos_ref, bf16[2,16,352,1024]{3,2,1,0:T(8,128)(2,1)} %bitcast.24, ...), custom_call_target="tpu_custom_call" | custom-call | flops 4000000000 | bytes 18874368 | tf_op jit(solution)/shard_map/pallas_call | solution.py:405
  137.2 0.0 collective-permute-start.3
  137.3 12.3 %shard_map.135 = (f32[128,512]{1,0:T(8,128)S(1)}, f32[128,512]{1,0:T(8,128)S(1)}) custom-call(s32[2,16,128]{2,1,0:T(8,128)S(1)} %get-tuple-element.30.off_ref, bf16[512,1024]{1,0:T(8,128)(2,1)S(1)} %bitcast.16, s32[2,8,512]{2,1,0:T(8,128)S(1)} %get-tuple-element.32.pos_ref, bf16[2,16,352,1024]{3,2,1,0:T(8,128)(2,1)} %bitcast.25, ...), custom_call_target="tpu_custom_call" | custom-call | flops 4000000000 | bytes 18874368 | tf_op jit(solution)/shard_map/pallas_call | solution.py:405
  149.6 11.4 %collective-permute-done.3.got_ref = f32[256,512]{1,0:T(8,128)S(1)} collective-permute-done((f32[256,512]{1,0:T(8,128)S(1)}, f32[256,512]{1,0:T(8,128)S(1)}, u32[]{:S(2)}, u32[]{:S(2)}) %collective-permute-start.3) | collective-permute-done | bytes 524320 | tf_op jit(solution)/shard_map/ppermute | solution.py:598
  160.9 5.0 %shard_map.137 = (bf16[3,512,768]{2,1,0:T(8,128)(2,1)S(1)}, f32[4,4,128,128]{3,2,1,0:T(8,128)S(1)}) custom-call(f32[256,512]{1,0:T(8,128)S(1)} %get-tuple-element.49.own_ref, f32[256,512]{1,0:T(8,128)S(1)} %collective-permute-done.3.got_ref, bf16[512,1024]{1,0:T(8,128)(2,1)S(1)} %bitcast.17, f32[2,64,1024]{2,1,0:T(8,128)S(1)} %bitcast.19, ...), custom_call_target="tpu_custom_call" | custom-call | flops 2000000000 | bytes 4194304 | tf_op jit(solution)/shard_map/pallas_call | solution.py:471
  165.9 0.0 collective-permute-done.2.got1_ref
  165.9 19.1 %shard_map.138 = bf16[128,1024]{1,0:T(8,128)(2,1)S(1)} custom-call(f32[384,512]{1,0:T(8,128)S(1)} %get-tuple-element.45.own1_ref, f32[384,512]{1,0:T(8,128)S(1)} %collective-permute-done.2.got1_ref, f32[128,512]{1,0:T(8,128)S(1)} %get-tuple-element.47.own2_ref, f32[128,512]{1,0:T(8,128)S(1)} %get-tuple-element.48.send2_ref, ...), custom_call_target="tpu_custom_call" | custom-call | tf_op jit(solution)/shard_map/pallas_call | solution.py:556
  185.0 0.7 copy.18
  (1 shorter events, 0.0 us)
Async XLA Ops:
  0.7 0.9 copy-start
  1.7 0.7 copy-start.1
  40.9 35.1 %collective-permute-start = (f32[384,512]{1,0:T(8,128)S(1)}, f32[384,512]{1,0:T(8,128)S(1)}, u32[]{:S(2)}, u32[]{:S(2)}) collective-permute-start(f32[384,512]{1,0:T(8,128)S(1)} %get-tuple-element.34), channel_id=1, source_target_pairs={{0,4},{4,0},{1,5},{5,1},{2,6},{6,2},{3,7},{7,3}} | collective-permute-start | bytes 2359304 | tf_op jit(solution)/shard_map/ppermute | solution.py:598
  46.9 24.1 %copy-start.3 = (f32[2,1024,64]{1,2,0:T(8,128)S(1)}, f32[2,1024,64]{1,2,0:T(8,128)}, u32[]{:S(2)}) copy-start(f32[2,1024,64]{1,2,0:T(8,128)} %param.21) | copy-start | bytes 1572868
  46.9 24.1 %collective-permute-start.1 = (f32[256,512]{1,0:T(8,128)S(1)}, f32[256,512]{1,0:T(8,128)S(1)}, u32[]{:S(2)}, u32[]{:S(2)}) collective-permute-start(f32[256,512]{1,0:T(8,128)S(1)} %get-tuple-element.38), channel_id=1, source_target_pairs={{0,4},{4,0},{1,5},{5,1},{2,6},{6,2},{3,7},{7,3}} | collective-permute-start | bytes 1572872 | tf_op jit(solution)/shard_map/ppermute | solution.py:598
  76.0 18.8 %copy-start.2 = (s32[128]{0:T(128)S(1)}, s32[128]{0:T(128)}, u32[]{:S(2)}) copy-start(s32[128]{0:T(128)} %len_ref.3) | copy-start | bytes 1540
  129.6 36.3 %collective-permute-start.2 = (f32[384,512]{1,0:T(8,128)S(1)}, f32[384,512]{1,0:T(8,128)S(1)}, u32[]{:S(2)}, u32[]{:S(2)}) collective-permute-start(f32[384,512]{1,0:T(8,128)S(1)} %get-tuple-element.46), channel_id=1, source_target_pairs={{0,4},{4,0},{1,5},{5,1},{2,6},{6,2},{3,7},{7,3}} | collective-permute-start | bytes 2359304 | tf_op jit(solution)/shard_map/ppermute | solution.py:598
  137.2 23.7 %collective-permute-start.3 = (f32[256,512]{1,0:T(8,128)S(1)}, f32[256,512]{1,0:T(8,128)S(1)}, u32[]{:S(2)}, u32[]{:S(2)}) collective-permute-start(f32[256,512]{1,0:T(8,128)S(1)} %get-tuple-element.50), channel_id=1, source_target_pairs={{0,4},{4,0},{1,5},{5,1},{2,6},{6,2},{3,7},{7,3}} | collective-permute-start | bytes 1572872 | tf_op jit(solution)/shard_map/ppermute | solution.py:598

commit v2 on v1

--- a/solution.py
+++ b/solution.py
@@ -20,7 +20,8 @@
 PART_ROWS = (256, 384, 128)
 PARTS = len(PART_ROWS)
 DEPTH = 4
-VMEM_MIB = (51, 51)
+VMEM_MIB = 51
+AHEAD = 12
 
 
 def _nn(a, b):
@@ -85,6 +86,11 @@
 
 
 def attn_kernel(layer, routed, x_ref, len_ref, k_hbm, v_hbm, wq_hbm, wk_hbm, wv_hbm, wo_hbm, *refs):
+    for _ in attn_steps(layer, routed, True, x_ref, len_ref, k_hbm, v_hbm, wq_hbm, wk_hbm, wv_hbm, wo_hbm, *refs):
+        pass
+
+
+def attn_steps(layer, routed, alone, x_ref, len_ref, k_hbm, v_hbm, wq_hbm, wk_hbm, wv_hbm, wo_hbm, *refs):
     if routed:
         ids_ref, *refs = refs
     u_all, a_out, a_recv, *refs = refs
@@ -95,7 +101,7 @@
     p, b, x, c, to_y, to_x, to_c = _where_am_i()
     half = x_ref.shape[0] // 2
     heads, dim = q3.shape[1], q3.shape[2]
-    rows = kbuf.shape[2]
+    slots, rows = kbuf.shape[0], kbuf.shape[2]
     n_half = half // TB
     n_blocks = 2 * n_half
     scale = dim ** -0.5
@@ -104,7 +110,7 @@
         return ((1 - p) + (n // n_half) * (2 * p - 1)) * half + (n % n_half) * TB
 
     def kv_copies(n):
-        slot = n % SLOTS
+        slot = n % slots
         src = pl.ds(tok_of(n), TB)
         return (pltpu.make_async_copy(k_hbm.at[layer, src], kbuf.at[slot], ksem.at[slot]),
                 pltpu.make_async_copy(v_hbm.at[layer, src], vbuf.at[slot], vsem.at[slot]))
@@ -112,11 +118,13 @@
     w_copies = [pltpu.make_async_copy(src.at[layer], dst, wsem.at[i])
                 for i, (src, dst) in enumerate(((wq_hbm, wq), (wk_hbm, wk), (wv_hbm, wv), (wo_hbm, wo)))]
     w_copies[0].start()
-    for n in range(SLOTS):
+    for n in range(slots):
         for cp in kv_copies(n):
             cp.start()
     for cp in w_copies[1:]:
         cp.start()
+
+    yield
 
     if routed:
         to_d = {"ep": (1 - x) * 2 + (1 - c)}
@@ -125,7 +133,7 @@
         id_copies = [_rcopy(ids_ref, idg.at[b], isend.at[i], irecv.at[i], peer) for i, peer in enumerate((to_x, to_c, to_d))]
         for cp in id_copies:
             cp.start()
-    else:
+    elif alone:
         _greet((to_y, to_x, to_c))
 
     normed = _rms(x_ref[...].astype(F32)).astype(BF16)
@@ -141,7 +149,7 @@
     lane = lax.broadcasted_iota(I32, (heads, 128), 1)
 
     def block(n, acc):
-        slot = n % SLOTS
+        slot = n % slots
         for cp in kv_copies(n):
             cp.wait()
         t0 = tok_of(n)
@@ -168,9 +176,9 @@
         acc = lax.fori_loop(0, 1, scores, acc)
         lax.fori_loop(0, 1, values, 0)
 
-        @pl.when(n + SLOTS < n_blocks)
+        @pl.when(n + slots < n_blocks)
         def _():
-            for cp in kv_copies(n + SLOTS):
+            for cp in kv_copies(n + slots):
                 cp.start()
 
         return acc
@@ -267,38 +275,43 @@
         cp.wait_send()
 
 
-def attention(layer, x, lens, kc, vc, wq, wk, wv, wo, ids=None, n_local=0):
+def attn_scratch(slots, tokens, rows, dim, wq):
+    d_model, heads, half = wq.shape[1], wq.shape[2] // dim, tokens // 2
+    dma = pltpu.SemaphoreType.DMA
+    weight = pltpu.VMEM(wq.shape[1:], BF16)
+    return [
+        pltpu.VMEM((slots, TB, rows, dim), BF16), pltpu.VMEM((slots, TB, rows, dim), BF16), pltpu.VMEM((TB, heads, rows), BF16),
+        weight, weight, weight, weight,
+        pltpu.VMEM((tokens, heads, dim), F32), pltpu.VMEM((tokens, heads, dim), F32), pltpu.VMEM((half, heads, dim), F32),
+        pltpu.VMEM((half, heads, dim), F32), pltpu.VMEM((half, heads, dim), F32),
+        pltpu.VMEM((heads, 128), F32), pltpu.VMEM((heads, 128), F32), pltpu.VMEM((half, heads * dim), BF16),
+        pltpu.VMEM((half, d_model), BF16),
+        dma((slots,)), dma((slots,)), dma((4,)), dma((half // TB + 1,)), dma((half // TB + 1,)), dma((11,)), dma((11,)),
+    ]
+
+
+def attention(layer, x, lens, kc, vc, wq, wk, wv, wo, ids, n_local):
     tokens, d_model = x.shape
     rows, dim = kc.shape[2], kc.shape[3]
-    heads = wq.shape[2] // dim
     half = tokens // 2
     hbm = pl.BlockSpec(memory_space=pltpu.HBM)
     vmem = pl.BlockSpec(memory_space=pltpu.VMEM)
     dma = pltpu.SemaphoreType.DMA
-    scratch = [
-        pltpu.VMEM((SLOTS, TB, rows, dim), BF16), pltpu.VMEM((SLOTS, TB, rows, dim), BF16), pltpu.VMEM((TB, heads, rows), BF16),
-        pltpu.VMEM(wq.shape[1:], BF16), pltpu.VMEM(wk.shape[1:], BF16), pltpu.VMEM(wv.shape[1:], BF16), pltpu.VMEM(wo.shape[1:], BF16),
-        pltpu.VMEM((tokens, heads, dim), F32), pltpu.VMEM((tokens, heads, dim), F32), pltpu.VMEM((half, heads, dim), F32),
-        pltpu.VMEM((half, heads, dim), F32), pltpu.VMEM((half, heads, dim), F32),
-        pltpu.VMEM((heads, 128), F32), pltpu.VMEM((heads, 128), F32), pltpu.VMEM((half, heads * dim), BF16),
-        pltpu.VMEM((half, d_model), BF16),
-        dma((SLOTS,)), dma((SLOTS,)), dma((4,)), dma((half // TB + 1,)), dma((half // TB + 1,)), dma((11,)), dma((11,)),
-    ]
+    scratch = attn_scratch(SLOTS, tokens, rows, dim, wq)
     out_shape = [jax.ShapeDtypeStruct((8, half, d_model), BF16)] + [jax.ShapeDtypeStruct((half, d_model // 2), BF16)] * 2
     in_specs = [vmem, pl.BlockSpec(memory_space=pltpu.SMEM)] + [hbm] * 6
     out_specs = [vmem] * 3
     args = [x, lens, kc, vc, wq, wk, wv, wo]
-    if ids is not None:
-        layers = ids.shape[0]
-        args.append(ids)
-        in_specs.append(vmem)
-        out_shape += [jax.ShapeDtypeStruct((layers, 8, 8 * half), I32)] * 2 + [jax.ShapeDtypeStruct((layers, n_local, 128), I32)]
-        out_specs += [vmem] * 3
-        scratch += [pltpu.VMEM((4,) + ids.shape, I32), dma((3,)), dma((3,))]
+    layers = ids.shape[0]
+    args.append(ids)
+    in_specs.append(vmem)
+    out_shape += [jax.ShapeDtypeStruct((layers, 8, 8 * half), I32)] * 2 + [jax.ShapeDtypeStruct((layers, n_local, 128), I32)]
+    out_specs += [vmem] * 3
+    scratch += [pltpu.VMEM((4,) + ids.shape, I32), dma((3,)), dma((3,))]
     u, a, a_got, *rest = pl.pallas_call(
-        functools.partial(attn_kernel, layer, ids is not None),
+        functools.partial(attn_kernel, layer, True),
         out_shape=out_shape, in_specs=in_specs, out_specs=out_specs, scratch_shapes=scratch,
-        compiler_params=pltpu.CompilerParams(collective_id=layer, has_side_effects=True, vmem_limit_bytes=VMEM_MIB[layer] << 20),
+        compiler_params=pltpu.CompilerParams(collective_id=layer, has_side_effects=True, vmem_limit_bytes=VMEM_MIB << 20),
     )(*args)
     return (u.reshape(8 * half, d_model), a, a_got, *rest)
 
@@ -478,8 +491,23 @@
     )(own, got, u, wr, ids, pos)
 
 
-def combine_kernel(own1_ref, got1_ref, own2_ref, send2_ref, gm, t0_ref, a_ref, a_got_ref, x_out,
-                   yr, tb, tcr, txs, txr, xo, a_buf, ysend, yrecv, csend, crecv, xsend, xrecv, fsend, frecv, lsem):
+def combine_kernel(*refs):
+    _combine(refs[:8], refs[8], refs[9:])
+
+
+def next_layer_kernel(layer, *refs):
+    inputs, operands, outs, scratch = refs[:8], refs[8:15], refs[15:18], refs[18:]
+    shared, mixing, attending = scratch[0], scratch[1:15], scratch[15:]
+    steps = attn_steps(layer, False, False, shared, *operands, *outs, *attending)
+    next(steps)
+    _combine(inputs, shared, mixing)
+    for _ in steps:
+        pass
+
+
+def _combine(inputs, xo, scratch):
+    own1_ref, got1_ref, own2_ref, send2_ref, gm, t0_ref, a_ref, a_got_ref = inputs
+    yr, tb, tcr, txs, txr, a_buf, ysend, yrecv, csend, crecv, xsend, xrecv, fsend, frecv = scratch
     p, _, x, c, to_y, to_x, to_c = _where_am_i()
     cw = yr.shape[2]
     mine = p * N_CH
@@ -537,35 +565,53 @@
             finish(j - 2)
     for copies in chunks:
         copies[-1].wait_recv()
-    out = pltpu.make_async_copy(xo, x_out, lsem)
-    out.start()
     for cp in y_copies:
         cp.wait_send()
     for copies in chunks:
         for cp in copies:
             cp.wait_send()
-    out.wait()
-
-
-def combine(layer, own1, got1, own2, send2, gm, t0, a, a_got):
+
+
+def combine_scratch(own2, t0, a):
     half, half_cols = a.shape
-    tokens = 2 * half
-    cw = half_cols // N_CH
+    tokens, cw = 2 * half, half_cols // N_CH
+    dma = pltpu.SemaphoreType.DMA
+    return [
+        pltpu.VMEM((N_CH, own2.shape[0], cw), F32), pltpu.VMEM(t0.shape, F32),
+        pltpu.VMEM((N_CH, 2, tokens, cw), F32), pltpu.VMEM((N_CH, tokens, cw), F32), pltpu.VMEM((N_CH, tokens, cw), F32),
+        pltpu.VMEM((tokens, half_cols), BF16),
+        dma((N_CH,)), dma((N_CH,)), dma((N_CH, 2)), dma((N_CH, 2)), dma((N_CH,)), dma((N_CH,)), dma((N_CH,)), dma((N_CH,)),
+    ]
+
+
+def combine(args):
+    half, half_cols = args[6].shape
     vmem = pl.BlockSpec(memory_space=pltpu.VMEM)
-    dma = pltpu.SemaphoreType.DMA
     return pl.pallas_call(
         combine_kernel,
-        out_shape=jax.ShapeDtypeStruct((tokens, 2 * half_cols), BF16),
+        out_shape=jax.ShapeDtypeStruct((2 * half, 2 * half_cols), BF16),
         in_specs=[vmem] * 8,
-        out_specs=pl.BlockSpec(memory_space=pl.ANY),
-        scratch_shapes=[
-            pltpu.VMEM((N_CH, own2.shape[0], cw), F32), pltpu.VMEM(t0.shape, F32),
-            pltpu.VMEM((N_CH, 2, tokens, cw), F32), pltpu.VMEM((N_CH, tokens, cw), F32), pltpu.VMEM((N_CH, tokens, cw), F32),
-            pltpu.VMEM((tokens, 2 * half_cols), BF16), pltpu.VMEM((tokens, half_cols), BF16),
-            dma((N_CH,)), dma((N_CH,)), dma((N_CH, 2)), dma((N_CH, 2)), dma((N_CH,)), dma((N_CH,)), dma((N_CH,)), dma((N_CH,)), dma,
-        ],
-        compiler_params=pltpu.CompilerParams(collective_id=2 + layer, has_side_effects=True, vmem_limit_bytes=32 << 20),
-    )(own1, got1, own2, send2, gm, t0, a, a_got)
+        out_specs=vmem,
+        scratch_shapes=combine_scratch(args[2], args[5], args[6]),
+        compiler_params=pltpu.CompilerParams(collective_id=8, has_side_effects=True, vmem_limit_bytes=32 << 20),
+    )(*args)
+
+
+def next_layer(layer, args, lens, kc, vc, wq, wk, wv, wo):
+    half, half_cols = args[6].shape
+    tokens, d_model = 2 * half, 2 * half_cols
+    vmem = pl.BlockSpec(memory_space=pltpu.VMEM)
+    hbm = pl.BlockSpec(memory_space=pltpu.HBM)
+    u, a, a_got = pl.pallas_call(
+        functools.partial(next_layer_kernel, layer),
+        out_shape=[jax.ShapeDtypeStruct((8, half, d_model), BF16)] + [jax.ShapeDtypeStruct((half, half_cols), BF16)] * 2,
+        in_specs=[vmem] * 8 + [pl.BlockSpec(memory_space=pltpu.SMEM)] + [hbm] * 6,
+        out_specs=[vmem] * 3,
+        scratch_shapes=[pltpu.VMEM((tokens, d_model), BF16)] + combine_scratch(args[2], args[5], args[6])
+        + attn_scratch(AHEAD, tokens, kc.shape[2], kc.shape[3], wq),
+        compiler_params=pltpu.CompilerParams(collective_id=layer, has_side_effects=True, vmem_limit_bytes=46 << 20),
+    )(*args, lens, kc, vc, wq, wk, wv, wo)
+    return u.reshape(8 * half, d_model), a, a_got
 
 
 def solution(mesh):
@@ -585,11 +631,9 @@
         w3 = jnp.swapaxes(w3, 2, 3)
         wr = jnp.swapaxes(wr, 1, 2)
         ids = jnp.pad(jnp.swapaxes(ids, 1, 2), ((0, 0), (0, 8 - top_k), (0, 0)))
+        weights = (lens, kc, vc, wq, wk, wv, wo)
+        u, a, a_got, pos, ids_all, off = attention(0, hidden, *weights, ids, n_local)
         for layer in range(layers):
-            first = layer == 0
-            u, a, a_got, *tables = attention(layer, hidden, lens, kc, vc, wq, wk, wv, wo, ids if first else None, n_local)
-            if first:
-                pos, ids_all, off = tables
             own, got = [], []
             for part in range(PARTS):
                 kept, send = experts(layer, part, off, u, pos, w1, w3, w2, PART_ROWS[part])
@@ -597,7 +641,9 @@
                 if part < PARTS - 1:
                     got.append(lax.ppermute(send, "pool", [(0, 1), (1, 0)]))
             gm, t0 = gates(layer, own[0], got[0], u, wr, ids_all, pos)
-            hidden = combine(layer, own[1], got[1], own[2], send, gm, t0, a, a_got)
-        return hidden
+            args = (own[1], got[1], own[2], send, gm, t0, a, a_got)
+            if layer + 1 < layers:
+                u, a, a_got = next_layer(layer + 1, args, *weights)
+        return combine(args)
 
     return jax.shard_map(body, mesh=mesh, in_specs=in_specs, out_specs=tok_spec, check_vma=False)

time: 186 us -> 183 us (0.984)
  Pallas kernels: 157 us -> 154 us
    pallas_call x4 -> x3, Pallas kernels: 91.1 us -> 87.8 us  [the longest x1 40.2 us: next_layer(): pl.pallas_call(functools.partial(next_layer_kernel, layer), out_shape=[ja...]
where the time goes in v2:
time: 183 us; the launch traced here: 182 us
  Pallas kernels  154 us (84%)
  waiting for transfers between devices  21.7 us (12%)
  starting transfers between devices  4.12 us (2%)
  local copies, waits for them, and re-layouts  3.02 us (2%)
    pallas_call x6, Pallas kernels, experts(): pl.pallas_call(functools.partial(expert_kernel, layer, part), out_shape=[...  55.7 us
    pallas_call x1, Pallas kernels, next_layer(): pl.pallas_call(functools.partial(next_layer_kernel, layer), out_shape=[ja...  40.2 us
    pallas_call x1, Pallas kernels, attention(): pl.pallas_call(functools.partial(attn_kernel, layer, True), out_shape=out...  28.6 us
    ppermute x4, waiting for transfers between devices, body(): got.append(lax.ppermute(send, 'pool', [(0, 1), (1, 0)]))  21.7 us
    pallas_call x1, Pallas kernels, combine(): pl.pallas_call(combine_kernel, out_shape=jax.ShapeDtypeStruct((2 * half,...  19.1 us
    pallas_call x2, Pallas kernels, gates(): pl.pallas_call(functools.partial(gate_kernel, layer), out_shape=[jax.Shap...  9.96 us
    ppermute x4, starting transfers between devices, body(): got.append(lax.ppermute(send, 'pool', [(0, 1), (1, 0)]))  4.12 us
  transfers between devices with their start and end apart: 4, of which 2 were waited for; matrix products, arithmetic and copies ran while one was open for 0% of the time, Pallas kernels for 25%

profile of v2, /device:TPU:0, one launch (start us, length us, event | category | flops | bytes accessed | tf_op | source)
XLA Modules:
  0.0 182.4 jit_solution(6549958372946856490)
XLA Ops:
  0.0 0.7 copy.16
  0.7 0.0 copy-start
  0.7 0.9 copy-done
  1.7 0.0 copy-start.1
  1.7 0.7 copy-done.1
  2.3 28.6 %shard_map.127 = (bf16[8,64,1024]{2,1,0:T(8,128)(2,1)S(1)}, bf16[64,512]{1,0:T(8,128)(2,1)S(1)}, bf16[64,512]{1,0:T(8,128)(2,1)S(1)}, s32[2,8,512]{2,1,0:T(8,128...) custom-call(bf16[128,1024]{1,0:T(8,128)(2,1)S(1)} %copy-done, s32[128]{0:T(128)S(1)} %copy-done.1, ...), custom_call_target="tpu_custom_call" | custom-call | tf_op jit(solution)/shard_map/pallas_call | solution.py:311
  30.9 10.0 %shard_map.128 = (f32[384,512]{1,0:T(8,128)S(1)}, f32[384,512]{1,0:T(8,128)S(1)}) custom-call(s32[2,16,128]{2,1,0:T(8,128)S(1)} %get-tuple-element.30.off_ref, bf16[512,1024]{1,0:T(8,128)(2,1)S(1)} %bitcast.14, s32[2,8,512]{2,1,0:T(8,128)S(1)} %get-tuple-element.32.pos_ref, bf16[2,16,352,1024]{3,2,1,0:T(8,128)(2,1)} %bitcast.20, ...), custom_call_target="tpu_custom_call" | custom-call | flops 4000000000 | bytes 18874368 | tf_op jit(solution)/shard_map/pallas_call | solution.py:418
  40.9 0.4 collective-permute-start
  41.3 5.6 %shard_map.130 = (f32[256,512]{1,0:T(8,128)S(1)}, f32[256,512]{1,0:T(8,128)S(1)}) custom-call(s32[2,16,128]{2,1,0:T(8,128)S(1)} %get-tuple-element.30.off_ref, bf16[512,1024]{1,0:T(8,128)(2,1)S(1)} %bitcast.15, s32[2,8,512]{2,1,0:T(8,128)S(1)} %get-tuple-element.32.pos_ref, bf16[2,16,352,1024]{3,2,1,0:T(8,128)(2,1)} %bitcast.21, ...), custom_call_target="tpu_custom_call" | custom-call | flops 4000000000 | bytes 18874368 | tf_op jit(solution)/shard_map/pallas_call | solution.py:418
  46.9 0.0 copy-start.2
  46.9 1.6 collective-permute-start.1
  48.6 12.2 %shard_map.129 = (f32[128,512]{1,0:T(8,128)S(1)}, f32[128,512]{1,0:T(8,128)S(1)}) custom-call(s32[2,16,128]{2,1,0:T(8,128)S(1)} %get-tuple-element.30.off_ref, bf16[512,1024]{1,0:T(8,128)(2,1)S(1)} %bitcast.16, s32[2,8,512]{2,1,0:T(8,128)S(1)} %get-tuple-element.32.pos_ref, bf16[2,16,352,1024]{3,2,1,0:T(8,128)(2,1)} %bitcast.22, ...), custom_call_target="tpu_custom_call" | custom-call | flops 4000000000 | bytes 18874368 | tf_op jit(solution)/shard_map/pallas_call | solution.py:418
  60.8 10.3 %collective-permute-done.1.got_ref = f32[256,512]{1,0:T(8,128)S(1)} collective-permute-done((f32[256,512]{1,0:T(8,128)S(1)}, f32[256,512]{1,0:T(8,128)S(1)}, u32[]{:S(2)}, u32[]{:S(2)}) %collective-permute-start.1) | collective-permute-done | bytes 524320 | tf_op jit(solution)/shard_map/ppermute | solution.py:642
  71.1 0.0 copy-done.2
  71.1 5.0 %shard_map.131 = (bf16[3,512,768]{2,1,0:T(8,128)(2,1)S(1)}, f32[4,4,128,128]{3,2,1,0:T(8,128)S(1)}) custom-call(f32[256,512]{1,0:T(8,128)S(1)} %get-tuple-element.37.own_ref, f32[256,512]{1,0:T(8,128)S(1)} %collective-permute-done.1.got_ref, bf16[512,1024]{1,0:T(8,128)(2,1)S(1)} %bitcast.17, f32[2,64,1024]{2,1,0:T(8,128)S(1)} %bitcast.18, ...), custom_call_target="tpu_custom_call" | custom-call | flops 2000000000 | bytes 4194304 | tf_op jit(solution)/shard_map/pallas_call | solution.py:484
  76.1 0.0 collective-permute-done.refs_1_
  76.1 40.2 %shard_map.132 = (bf16[8,64,1024]{2,1,0:T(8,128)(2,1)S(1)}, bf16[64,512]{1,0:T(8,128)(2,1)S(1)}, bf16[64,512]{1,0:T(8,128)(2,1)S(1)}) custom-call(f32[384,512]{1,0:T(8,128)S(1)} %get-tuple-element.33.refs_0_, f32[384,512]{1,0:T(8,128)S(1)} %collective-permute-done.refs_1_, f32[128,512]{1,0:T(8,128)S(1)} %get-tuple-element.35.refs_2_, ...), custom_call_target="tpu_custom_call" | custom-call | tf_op jit(solution)/shard_map/pallas_call | solution.py:605
  116.3 10.0 %shard_map.133 = (f32[384,512]{1,0:T(8,128)S(1)}, f32[384,512]{1,0:T(8,128)S(1)}) custom-call(s32[2,16,128]{2,1,0:T(8,128)S(1)} %get-tuple-element.30.off_ref, bf16[512,1024]{1,0:T(8,128)(2,1)S(1)} %bitcast.10, s32[2,8,512]{2,1,0:T(8,128)S(1)} %get-tuple-element.32.pos_ref, bf16[2,16,352,1024]{3,2,1,0:T(8,128)(2,1)} %bitcast.23, ...), custom_call_target="tpu_custom_call" | custom-call | flops 4000000000 | bytes 18874368 | tf_op jit(solution)/shard_map/pallas_call | solution.py:418
  126.3 2.0 %collective-permute-start.2 = (f32[384,512]{1,0:T(8,128)S(1)}, f32[384,512]{1,0:T(8,128)S(1)}, u32[]{:S(2)}, u32[]{:S(2)}) collective-permute-start(f32[384,512]{1,0:T(8,128)S(1)} %get-tuple-element.46), channel_id=1, source_target_pairs={{0,4},{4,0},{1,5},{5,1},{2,6},{6,2},{3,7},{7,3}} | collective-permute-start | bytes 2359304 | tf_op jit(solution)/shard_map/ppermute | solution.py:642
  128.3 5.6 %shard_map.135 = (f32[256,512]{1,0:T(8,128)S(1)}, f32[256,512]{1,0:T(8,128)S(1)}) custom-call(s32[2,16,128]{2,1,0:T(8,128)S(1)} %get-tuple-element.30.off_ref, bf16[512,1024]{1,0:T(8,128)(2,1)S(1)} %bitcast.11, s32[2,8,512]{2,1,0:T(8,128)S(1)} %get-tuple-element.32.pos_ref, bf16[2,16,352,1024]{3,2,1,0:T(8,128)(2,1)} %bitcast.24, ...), custom_call_target="tpu_custom_call" | custom-call | flops 4000000000 | bytes 18874368 | tf_op jit(solution)/shard_map/pallas_call | solution.py:418
  134.0 0.1 collective-permute-start.3
  134.0 12.3 %shard_map.134 = (f32[128,512]{1,0:T(8,128)S(1)}, f32[128,512]{1,0:T(8,128)S(1)}) custom-call(s32[2,16,128]{2,1,0:T(8,128)S(1)} %get-tuple-element.30.off_ref, bf16[512,1024]{1,0:T(8,128)(2,1)S(1)} %bitcast.12, s32[2,8,512]{2,1,0:T(8,128)S(1)} %get-tuple-element.32.pos_ref, bf16[2,16,352,1024]{3,2,1,0:T(8,128)(2,1)} %bitcast.25, ...), custom_call_target="tpu_custom_call" | custom-call | flops 4000000000 | bytes 18874368 | tf_op jit(solution)/shard_map/pallas_call | solution.py:418
  146.3 11.4 %collective-permute-done.3.got_ref = f32[256,512]{1,0:T(8,128)S(1)} collective-permute-done((f32[256,512]{1,0:T(8,128)S(1)}, f32[256,512]{1,0:T(8,128)S(1)}, u32[]{:S(2)}, u32[]{:S(2)}) %collective-permute-start.3) | collective-permute-done | bytes 524320 | tf_op jit(solution)/shard_map/ppermute | solution.py:642
  157.7 5.0 %shard_map.136 = (bf16[3,512,768]{2,1,0:T(8,128)(2,1)S(1)}, f32[4,4,128,128]{3,2,1,0:T(8,128)S(1)}) custom-call(f32[256,512]{1,0:T(8,128)S(1)} %get-tuple-element.49.own_ref, f32[256,512]{1,0:T(8,128)S(1)} %collective-permute-done.3.got_ref, bf16[512,1024]{1,0:T(8,128)(2,1)S(1)} %bitcast.13, f32[2,64,1024]{2,1,0:T(8,128)S(1)} %bitcast.19, ...), custom_call_target="tpu_custom_call" | custom-call | flops 2000000000 | bytes 4194304 | tf_op jit(solution)/shard_map/pallas_call | solution.py:484
  162.7 0.0 collective-permute-done.2.refs_1_
  162.7 19.1 %shard_map.137 = bf16[128,1024]{1,0:T(8,128)(2,1)S(1)} custom-call(f32[384,512]{1,0:T(8,128)S(1)} %get-tuple-element.45.refs_0_, f32[384,512]{1,0:T(8,128)S(1)} %collective-permute-done.2.refs_1_, f32[128,512]{1,0:T(8,128)S(1)} %get-tuple-element.47.refs_2_, f32[128,512]{1,0:T(8,128)S(1)} %get-tuple-element.48.refs_3_, ...), custom_call_target="tpu_custom_call" | custom-call | tf_op jit(solution)/shard_map/pallas_call | solution.py:590
  181.7 0.7 copy.18
  (1 shorter events, 0.0 us)
Async XLA Ops:
  0.7 0.9 copy-start
  1.7 0.7 copy-start.1
  40.9 35.1 %collective-permute-start = (f32[384,512]{1,0:T(8,128)S(1)}, f32[384,512]{1,0:T(8,128)S(1)}, u32[]{:S(2)}, u32[]{:S(2)}) collective-permute-start(f32[384,512]{1,0:T(8,128)S(1)} %get-tuple-element.34), channel_id=1, source_target_pairs={{0,4},{4,0},{1,5},{5,1},{2,6},{6,2},{3,7},{7,3}} | collective-permute-start | bytes 2359304 | tf_op jit(solution)/shard_map/ppermute | solution.py:642
  46.9 24.1 %copy-start.2 = (f32[2,1024,64]{1,2,0:T(8,128)S(1)}, f32[2,1024,64]{1,2,0:T(8,128)}, u32[]{:S(2)}) copy-start(f32[2,1024,64]{1,2,0:T(8,128)} %param.21) | copy-start | bytes 1572868
  46.9 24.1 %collective-permute-start.1 = (f32[256,512]{1,0:T(8,128)S(1)}, f32[256,512]{1,0:T(8,128)S(1)}, u32[]{:S(2)}, u32[]{:S(2)}) collective-permute-start(f32[256,512]{1,0:T(8,128)S(1)} %get-tuple-element.38), channel_id=1, source_target_pairs={{0,4},{4,0},{1,5},{5,1},{2,6},{6,2},{3,7},{7,3}} | collective-permute-start | bytes 1572872 | tf_op jit(solution)/shard_map/ppermute | solution.py:642
  126.3 36.3 %collective-permute-start.2 = (f32[384,512]{1,0:T(8,128)S(1)}, f32[384,512]{1,0:T(8,128)S(1)}, u32[]{:S(2)}, u32[]{:S(2)}) collective-permute-start(f32[384,512]{1,0:T(8,128)S(1)} %get-tuple-element.46), channel_id=1, source_target_pairs={{0,4},{4,0},{1,5},{5,1},{2,6},{6,2},{3,7},{7,3}} | collective-permute-start | bytes 2359304 | tf_op jit(solution)/shard_map/ppermute | solution.py:642
  134.0 23.7 %collective-permute-start.3 = (f32[256,512]{1,0:T(8,128)S(1)}, f32[256,512]{1,0:T(8,128)S(1)}, u32[]{:S(2)}, u32[]{:S(2)}) collective-permute-start(f32[256,512]{1,0:T(8,128)S(1)} %get-tuple-element.50), channel_id=1, source_target_pairs={{0,4},{4,0},{1,5},{5,1},{2,6},{6,2},{3,7},{7,3}} | collective-permute-start | bytes 1572872 | tf_op jit(solution)/shard_map/ppermute | solution.py:642

commit v3 on v2

--- a/solution.py
+++ b/solution.py
@@ -148,38 +148,48 @@
     posl = jnp.where(lane_i % heads == row_i, lane_i // heads + p * (rows // heads), 1 << 20)
     lane = lax.broadcasted_iota(I32, (heads, 128), 1)
 
-    def block(n, acc):
-        slot = n % slots
-        for cp in kv_copies(n):
-            cp.wait()
-        t0 = tok_of(n)
+    group = pbuf.shape[0] // TB
+
+    def block(i, acc):
+        for g in range(group):
+            for cp in kv_copies(i * group + g):
+                cp.wait()
 
         def scores(_, acc):
-            for j in range(TB):
-                q = q3[t0 + j].astype(BF16)
-                s = _nt(q, kbuf[slot, j])
-                s = jnp.where(posl < len_ref[t0 + j], s * scale, NEG)
-                m = jnp.max(s, axis=1, keepdims=True)
-                pr = jnp.exp(s - m)
-                l = jnp.sum(pr, axis=1, keepdims=True)
-                pbuf[j] = pr.astype(BF16)
-                at = (n % n_half) * TB + j
-                acc = jnp.where(lane == at, m, acc)
-                acc = jnp.where(lane == half + at, l, acc)
+            for g in range(group):
+                n = i * group + g
+                t0 = tok_of(n)
+                for j in range(TB):
+                    q = q3[t0 + j].astype(BF16)
+                    s = _nt(q, kbuf[n % slots, j])
+                    s = jnp.where(posl < len_ref[t0 + j], s * scale, NEG)
+                    m = jnp.max(s, axis=1, keepdims=True)
+                    pr = jnp.exp(s - m)
+                    l = jnp.sum(pr, axis=1, keepdims=True)
+                    pbuf[g * TB + j] = pr.astype(BF16)
+                    at = (n % n_half) * TB + j
+                    acc = jnp.where(lane == at, m, acc)
+                    acc = jnp.where(lane == half + at, l, acc)
             return acc
 
         def values(_, none):
-            for j in range(TB):
-                o3[t0 + j] = _nn(pbuf[j], vbuf[slot, j])
+            for g in range(group):
+                n = i * group + g
+                t0 = tok_of(n)
+                for j in range(TB):
+                    o3[t0 + j] = _nn(pbuf[g * TB + j], vbuf[n % slots, j])
             return none
 
         acc = lax.fori_loop(0, 1, scores, acc)
         lax.fori_loop(0, 1, values, 0)
 
-        @pl.when(n + slots < n_blocks)
-        def _():
-            for cp in kv_copies(n + slots):
-                cp.start()
+        for g in range(group):
+            n = i * group + g
+
+            @pl.when(n + slots < n_blocks)
+            def _(n=n):
+                for cp in kv_copies(n + slots):
+                    cp.start()
 
         return acc
 
@@ -189,13 +199,14 @@
     def o_copy(i):
         return _rcopy(o3.at[pl.ds(theirs + i * TB, TB)], o3r.at[pl.ds(i * TB, TB)], osend.at[i], orecv.at[i], to_y)
 
-    def first(n, acc):
-        acc = block(n, acc)
-        o_copy(n).start()
+    def first(i, acc):
+        acc = block(i, acc)
+        for g in range(group):
+            o_copy(i * group + g).start()
         return acc
 
     zero = jnp.zeros((heads, 128), F32)
-    mls[...] = lax.fori_loop(0, n_half, first, zero)
+    mls[...] = lax.fori_loop(0, n_half // group, first, zero)
     ml_copy = _rcopy(mls, mlr, osend.at[n_half], orecv.at[n_half], to_y)
     ml_copy.start()
     normed = _rms(x_ref[pl.ds(mine, half), :].astype(F32)).astype(BF16)
@@ -215,7 +226,7 @@
             cp.wait()
         _route(b, idg, pos_out, ids_out, off_out)
 
-    ml_own = lax.fori_loop(n_half, n_blocks, block, zero)
+    ml_own = lax.fori_loop(n_half // group, n_blocks // group, block, zero)
 
     for i in range(n_half):
         o_copy(i).wait()
@@ -275,12 +286,12 @@
         cp.wait_send()
 
 
-def attn_scratch(slots, tokens, rows, dim, wq):
+def attn_scratch(slots, group, tokens, rows, dim, wq):
     d_model, heads, half = wq.shape[1], wq.shape[2] // dim, tokens // 2
     dma = pltpu.SemaphoreType.DMA
     weight = pltpu.VMEM(wq.shape[1:], BF16)
     return [
-        pltpu.VMEM((slots, TB, rows, dim), BF16), pltpu.VMEM((slots, TB, rows, dim), BF16), pltpu.VMEM((TB, heads, rows), BF16),
+        pltpu.VMEM((slots, TB, rows, dim), BF16), pltpu.VMEM((slots, TB, rows, dim), BF16), pltpu.VMEM((group * TB, heads, rows), BF16),
         weight, weight, weight, weight,
         pltpu.VMEM((tokens, heads, dim), F32), pltpu.VMEM((tokens, heads, dim), F32), pltpu.VMEM((half, heads, dim), F32),
         pltpu.VMEM((half, heads, dim), F32), pltpu.VMEM((half, heads, dim), F32),
@@ -297,7 +308,7 @@
     hbm = pl.BlockSpec(memory_space=pltpu.HBM)
     vmem = pl.BlockSpec(memory_space=pltpu.VMEM)
     dma = pltpu.SemaphoreType.DMA
-    scratch = attn_scratch(SLOTS, tokens, rows, dim, wq)
+    scratch = attn_scratch(SLOTS, 1, tokens, rows, dim, wq)
     out_shape = [jax.ShapeDtypeStruct((8, half, d_model), BF16)] + [jax.ShapeDtypeStruct((half, d_model // 2), BF16)] * 2
     in_specs = [vmem, pl.BlockSpec(memory_space=pltpu.SMEM)] + [hbm] * 6
     out_specs = [vmem] * 3
@@ -608,7 +619,7 @@
         in_specs=[vmem] * 8 + [pl.BlockSpec(memory_space=pltpu.SMEM)] + [hbm] * 6,
         out_specs=[vmem] * 3,
         scratch_shapes=[pltpu.VMEM((tokens, d_model), BF16)] + combine_scratch(args[2], args[5], args[6])
-        + attn_scratch(AHEAD, tokens, kc.shape[2], kc.shape[3], wq),
+        + attn_scratch(AHEAD, 2, tokens, kc.shape[2], kc.shape[3], wq),
         compiler_params=pltpu.CompilerParams(collective_id=layer, has_side_effects=True, vmem_limit_bytes=46 << 20),
     )(*args, lens, kc, vc, wq, wk, wv, wo)
     return u.reshape(8 * half, d_model), a, a_got

time: 183 us -> 181 us (0.989)
  Pallas kernels: 154 us -> 152 us
    pallas_call x1, Pallas kernels: 40.2 us -> 38.2 us  [next_layer(): pl.pallas_call(functools.partial(next_layer_kernel, layer), out_shape=[ja...]
where the time goes in v3:
time: 181 us; the launch traced here: 180 us
  Pallas kernels  152 us (84%)
  waiting for transfers between devices  21.7 us (12%)
  starting transfers between devices  4.13 us (2%)
  local copies, waits for them, and re-layouts  3.02 us (2%)
    pallas_call x6, Pallas kernels, experts(): pl.pallas_call(functools.partial(expert_kernel, layer, part), out_shape=[...  55.7 us
    pallas_call x1, Pallas kernels, next_layer(): pl.pallas_call(functools.partial(next_layer_kernel, layer), out_shape=[ja...  38.2 us
    pallas_call x1, Pallas kernels, attention(): pl.pallas_call(functools.partial(attn_kernel, layer, True), out_shape=out...  28.6 us
    ppermute x4, waiting for transfers between devices, body(): got.append(lax.ppermute(send, 'pool', [(0, 1), (1, 0)]))  21.7 us
    pallas_call x1, Pallas kernels, combine(): pl.pallas_call(combine_kernel, out_shape=jax.ShapeDtypeStruct((2 * half,...  19.1 us
    pallas_call x2, Pallas kernels, gates(): pl.pallas_call(functools.partial(gate_kernel, layer), out_shape=[jax.Shap...  9.96 us
    ppermute x4, starting transfers between devices, body(): got.append(lax.ppermute(send, 'pool', [(0, 1), (1, 0)]))  4.13 us
  transfers between devices with their start and end apart: 4, of which 2 were waited for; matrix products, arithmetic and copies ran while one was open for 0% of the time, Pallas kernels for 25%

profile of v3, /device:TPU:0, one launch (start us, length us, event | category | flops | bytes accessed | tf_op | source)
XLA Modules:
  0.0 180.5 jit_solution(4499301406388945108)
XLA Ops:
  0.0 0.7 copy.16
  0.7 0.0 copy-start
  0.7 0.9 copy-done
  1.7 0.0 copy-start.1
  1.7 0.7 copy-done.1
  2.3 28.6 %shard_map.127 = (bf16[8,64,1024]{2,1,0:T(8,128)(2,1)S(1)}, bf16[64,512]{1,0:T(8,128)(2,1)S(1)}, bf16[64,512]{1,0:T(8,128)(2,1)S(1)}, s32[2,8,512]{2,1,0:T(8,128...) custom-call(bf16[128,1024]{1,0:T(8,128)(2,1)S(1)} %copy-done, s32[128]{0:T(128)S(1)} %copy-done.1, ...), custom_call_target="tpu_custom_call" | custom-call | tf_op jit(solution)/shard_map/pallas_call | solution.py:322
  30.9 10.0 %shard_map.128 = (f32[384,512]{1,0:T(8,128)S(1)}, f32[384,512]{1,0:T(8,128)S(1)}) custom-call(s32[2,16,128]{2,1,0:T(8,128)S(1)} %get-tuple-element.30.off_ref, bf16[512,1024]{1,0:T(8,128)(2,1)S(1)} %bitcast.14, s32[2,8,512]{2,1,0:T(8,128)S(1)} %get-tuple-element.32.pos_ref, bf16[2,16,352,1024]{3,2,1,0:T(8,128)(2,1)} %bitcast.20, ...), custom_call_target="tpu_custom_call" | custom-call | flops 4000000000 | bytes 18874368 | tf_op jit(solution)/shard_map/pallas_call | solution.py:429
  40.9 0.4 collective-permute-start
  41.3 5.6 %shard_map.130 = (f32[256,512]{1,0:T(8,128)S(1)}, f32[256,512]{1,0:T(8,128)S(1)}) custom-call(s32[2,16,128]{2,1,0:T(8,128)S(1)} %get-tuple-element.30.off_ref, bf16[512,1024]{1,0:T(8,128)(2,1)S(1)} %bitcast.15, s32[2,8,512]{2,1,0:T(8,128)S(1)} %get-tuple-element.32.pos_ref, bf16[2,16,352,1024]{3,2,1,0:T(8,128)(2,1)} %bitcast.21, ...), custom_call_target="tpu_custom_call" | custom-call | flops 4000000000 | bytes 18874368 | tf_op jit(solution)/shard_map/pallas_call | solution.py:429
  46.9 0.0 copy-start.2
  46.9 1.6 collective-permute-start.1
  48.6 12.2 %shard_map.129 = (f32[128,512]{1,0:T(8,128)S(1)}, f32[128,512]{1,0:T(8,128)S(1)}) custom-call(s32[2,16,128]{2,1,0:T(8,128)S(1)} %get-tuple-element.30.off_ref, bf16[512,1024]{1,0:T(8,128)(2,1)S(1)} %bitcast.16, s32[2,8,512]{2,1,0:T(8,128)S(1)} %get-tuple-element.32.pos_ref, bf16[2,16,352,1024]{3,2,1,0:T(8,128)(2,1)} %bitcast.22, ...), custom_call_target="tpu_custom_call" | custom-call | flops 4000000000 | bytes 18874368 | tf_op jit(solution)/shard_map/pallas_call | solution.py:429
  60.8 10.3 %collective-permute-done.1.got_ref = f32[256,512]{1,0:T(8,128)S(1)} collective-permute-done((f32[256,512]{1,0:T(8,128)S(1)}, f32[256,512]{1,0:T(8,128)S(1)}, u32[]{:S(2)}, u32[]{:S(2)}) %collective-permute-start.1) | collective-permute-done | bytes 524320 | tf_op jit(solution)/shard_map/ppermute | solution.py:653
  71.1 0.0 copy-done.2
  71.1 5.0 %shard_map.131 = (bf16[3,512,768]{2,1,0:T(8,128)(2,1)S(1)}, f32[4,4,128,128]{3,2,1,0:T(8,128)S(1)}) custom-call(f32[256,512]{1,0:T(8,128)S(1)} %get-tuple-element.37.own_ref, f32[256,512]{1,0:T(8,128)S(1)} %collective-permute-done.1.got_ref, bf16[512,1024]{1,0:T(8,128)(2,1)S(1)} %bitcast.17, f32[2,64,1024]{2,1,0:T(8,128)S(1)} %bitcast.18, ...), custom_call_target="tpu_custom_call" | custom-call | flops 2000000000 | bytes 4194304 | tf_op jit(solution)/shard_map/pallas_call | solution.py:495
  76.1 0.0 collective-permute-done.refs_1_
  76.1 38.2 %shard_map.132 = (bf16[8,64,1024]{2,1,0:T(8,128)(2,1)S(1)}, bf16[64,512]{1,0:T(8,128)(2,1)S(1)}, bf16[64,512]{1,0:T(8,128)(2,1)S(1)}) custom-call(f32[384,512]{1,0:T(8,128)S(1)} %get-tuple-element.33.refs_0_, f32[384,512]{1,0:T(8,128)S(1)} %collective-permute-done.refs_1_, f32[128,512]{1,0:T(8,128)S(1)} %get-tuple-element.35.refs_2_, ...), custom_call_target="tpu_custom_call" | custom-call | tf_op jit(solution)/shard_map/pallas_call | solution.py:616
  114.3 10.0 %shard_map.133 = (f32[384,512]{1,0:T(8,128)S(1)}, f32[384,512]{1,0:T(8,128)S(1)}) custom-call(s32[2,16,128]{2,1,0:T(8,128)S(1)} %get-tuple-element.30.off_ref, bf16[512,1024]{1,0:T(8,128)(2,1)S(1)} %bitcast.10, s32[2,8,512]{2,1,0:T(8,128)S(1)} %get-tuple-element.32.pos_ref, bf16[2,16,352,1024]{3,2,1,0:T(8,128)(2,1)} %bitcast.23, ...), custom_call_target="tpu_custom_call" | custom-call | flops 4000000000 | bytes 18874368 | tf_op jit(solution)/shard_map/pallas_call | solution.py:429
  124.3 2.0 %collective-permute-start.2 = (f32[384,512]{1,0:T(8,128)S(1)}, f32[384,512]{1,0:T(8,128)S(1)}, u32[]{:S(2)}, u32[]{:S(2)}) collective-permute-start(f32[384,512]{1,0:T(8,128)S(1)} %get-tuple-element.46), channel_id=1, source_target_pairs={{0,4},{4,0},{1,5},{5,1},{2,6},{6,2},{3,7},{7,3}} | collective-permute-start | bytes 2359304 | tf_op jit(solution)/shard_map/ppermute | solution.py:653
  126.4 5.8 %shard_map.135 = (f32[256,512]{1,0:T(8,128)S(1)}, f32[256,512]{1,0:T(8,128)S(1)}) custom-call(s32[2,16,128]{2,1,0:T(8,128)S(1)} %get-tuple-element.30.off_ref, bf16[512,1024]{1,0:T(8,128)(2,1)S(1)} %bitcast.11, s32[2,8,512]{2,1,0:T(8,128)S(1)} %get-tuple-element.32.pos_ref, bf16[2,16,352,1024]{3,2,1,0:T(8,128)(2,1)} %bitcast.24, ...), custom_call_target="tpu_custom_call" | custom-call | flops 4000000000 | bytes 18874368 | tf_op jit(solution)/shard_map/pallas_call | solution.py:429
  132.2 0.0 collective-permute-start.3
  132.3 12.1 %shard_map.134 = (f32[128,512]{1,0:T(8,128)S(1)}, f32[128,512]{1,0:T(8,128)S(1)}) custom-call(s32[2,16,128]{2,1,0:T(8,128)S(1)} %get-tuple-element.30.off_ref, bf16[512,1024]{1,0:T(8,128)(2,1)S(1)} %bitcast.12, s32[2,8,512]{2,1,0:T(8,128)S(1)} %get-tuple-element.32.pos_ref, bf16[2,16,352,1024]{3,2,1,0:T(8,128)(2,1)} %bitcast.25, ...), custom_call_target="tpu_custom_call" | custom-call | flops 4000000000 | bytes 18874368 | tf_op jit(solution)/shard_map/pallas_call | solution.py:429
  144.3 11.4 %collective-permute-done.3.got_ref = f32[256,512]{1,0:T(8,128)S(1)} collective-permute-done((f32[256,512]{1,0:T(8,128)S(1)}, f32[256,512]{1,0:T(8,128)S(1)}, u32[]{:S(2)}, u32[]{:S(2)}) %collective-permute-start.3) | collective-permute-done | bytes 524320 | tf_op jit(solution)/shard_map/ppermute | solution.py:653
  155.7 5.0 %shard_map.136 = (bf16[3,512,768]{2,1,0:T(8,128)(2,1)S(1)}, f32[4,4,128,128]{3,2,1,0:T(8,128)S(1)}) custom-call(f32[256,512]{1,0:T(8,128)S(1)} %get-tuple-element.49.own_ref, f32[256,512]{1,0:T(8,128)S(1)} %collective-permute-done.3.got_ref, bf16[512,1024]{1,0:T(8,128)(2,1)S(1)} %bitcast.13, f32[2,64,1024]{2,1,0:T(8,128)S(1)} %bitcast.19, ...), custom_call_target="tpu_custom_call" | custom-call | flops 2000000000 | bytes 4194304 | tf_op jit(solution)/shard_map/pallas_call | solution.py:495
  160.7 0.0 collective-permute-done.2.refs_1_
  160.7 19.1 %shard_map.137 = bf16[128,1024]{1,0:T(8,128)(2,1)S(1)} custom-call(f32[384,512]{1,0:T(8,128)S(1)} %get-tuple-element.45.refs_0_, f32[384,512]{1,0:T(8,128)S(1)} %collective-permute-done.2.refs_1_, f32[128,512]{1,0:T(8,128)S(1)} %get-tuple-element.47.refs_2_, f32[128,512]{1,0:T(8,128)S(1)} %get-tuple-element.48.refs_3_, ...), custom_call_target="tpu_custom_call" | custom-call | tf_op jit(solution)/shard_map/pallas_call | solution.py:601
  179.8 0.7 copy.18
  (1 shorter events, 0.0 us)
Async XLA Ops:
  0.7 0.9 copy-start
  1.7 0.7 copy-start.1
  40.9 35.1 %collective-permute-start = (f32[384,512]{1,0:T(8,128)S(1)}, f32[384,512]{1,0:T(8,128)S(1)}, u32[]{:S(2)}, u32[]{:S(2)}) collective-permute-start(f32[384,512]{1,0:T(8,128)S(1)} %get-tuple-element.34), channel_id=1, source_target_pairs={{0,4},{4,0},{1,5},{5,1},{2,6},{6,2},{3,7},{7,3}} | collective-permute-start | bytes 2359304 | tf_op jit(solution)/shard_map/ppermute | solution.py:653
  46.9 24.1 %copy-start.2 = (f32[2,1024,64]{1,2,0:T(8,128)S(1)}, f32[2,1024,64]{1,2,0:T(8,128)}, u32[]{:S(2)}) copy-start(f32[2,1024,64]{1,2,0:T(8,128)} %param.21) | copy-start | bytes 1572868
  46.9 24.1 %collective-permute-start.1 = (f32[256,512]{1,0:T(8,128)S(1)}, f32[256,512]{1,0:T(8,128)S(1)}, u32[]{:S(2)}, u32[]{:S(2)}) collective-permute-start(f32[256,512]{1,0:T(8,128)S(1)} %get-tuple-element.38), channel_id=1, source_target_pairs={{0,4},{4,0},{1,5},{5,1},{2,6},{6,2},{3,7},{7,3}} | collective-permute-start | bytes 1572872 | tf_op jit(solution)/shard_map/ppermute | solution.py:653
  124.3 36.3 %collective-permute-start.2 = (f32[384,512]{1,0:T(8,128)S(1)}, f32[384,512]{1,0:T(8,128)S(1)}, u32[]{:S(2)}, u32[]{:S(2)}) collective-permute-start(f32[384,512]{1,0:T(8,128)S(1)} %get-tuple-element.46), channel_id=1, source_target_pairs={{0,4},{4,0},{1,5},{5,1},{2,6},{6,2},{3,7},{7,3}} | collective-permute-start | bytes 2359304 | tf_op jit(solution)/shard_map/ppermute | solution.py:653
  132.2 23.5 %collective-permute-start.3 = (f32[256,512]{1,0:T(8,128)S(1)}, f32[256,512]{1,0:T(8,128)S(1)}, u32[]{:S(2)}, u32[]{:S(2)}) collective-permute-start(f32[256,512]{1,0:T(8,128)S(1)} %get-tuple-element.50), channel_id=1, source_target_pairs={{0,4},{4,0},{1,5},{5,1},{2,6},{6,2},{3,7},{7,3}} | collective-permute-start | bytes 1572872 | tf_op jit(solution)/shard_map/ppermute | solution.py:653

commit v4 on v3

--- a/solution.py
+++ b/solution.py
@@ -255,34 +255,44 @@
         ref = u_all.at[src] if part is None else u_all.at[src, part]
         return _rcopy(ref, ref, gsend.at[i], grecv.at[i], peer)
 
-    own_y = [u_copy(0, me, to_y, lo), u_copy(1, me, to_y, hi)]
-    own_x = [u_copy(2, me, to_x, hi), u_copy(3, me, to_x, lo)]
-    own_c = u_copy(4, me, to_c)
-    for cp in (own_y[0], own_x[0], own_y[1], own_x[1], own_c):
-        cp.start()
+    quarter = [pl.ds(k * (half // 4), half // 4) for k in range(4)]
+    own_y = [u_copy(k, me, to_y, quarter[k]) for k in range(4)]
+    own_x = [u_copy(4 + k, me, to_x, quarter[k]) for k in range(4)]
+    own_c = u_copy(8, me, to_c)
+    for k in range(4):
+        own_y[k].start()
+        own_x[(k + 2) % 4].start()
+    own_c.start()
     cw = d_model // 2
     a_out[...] = a_own[:, pl.ds(pl.multiple_of(p * cw, 128), cw)]
-    a_copy = _rcopy(a_own.at[:, pl.ds(pl.multiple_of((1 - p) * cw, 128), cw)], a_recv, gsend.at[10], grecv.at[10], to_y)
-    own_y[0].wait_recv()
-    fwd_x = u_copy(5, y_blk, to_x, lo)
-    fwd_x.start()
+    a_copy = _rcopy(a_own.at[:, pl.ds(pl.multiple_of((1 - p) * cw, 128), cw)], a_recv, gsend.at[9], grecv.at[9], to_y)
+    fwd_x = [u_copy(10 + k, y_blk, to_x, quarter[k]) for k in range(2)]
+    fwd_y = [u_copy(12 + k, x_blk, to_y, quarter[2 + k]) for k in range(2)]
+    for k in range(2):
+        own_y[k].wait_recv()
+        fwd_x[k].start()
+        own_x[2 + k].wait_recv()
+        fwd_y[k].start()
+    a_copy.start()
+    own_y[2].wait_recv()
+    own_y[3].wait_recv()
+    c_y = u_copy(14, y_blk, to_c)
+    c_y.start()
     own_x[0].wait_recv()
-    fwd_y = u_copy(6, x_blk, to_y, hi)
-    fwd_y.start()
-    a_copy.start()
-    own_y[1].wait_recv()
-    c_y = u_copy(7, y_blk, to_c)
-    c_y.start()
     own_x[1].wait_recv()
-    c_x = u_copy(8, x_blk, to_c)
+    c_x = u_copy(15, x_blk, to_c)
     c_x.start()
-    fwd_x.wait_recv()
-    fwd_y.wait_recv()
-    c_d = u_copy(9, d_blk, to_c)
-    c_d.start()
-    for cp in (own_c, c_y, c_x, c_d, a_copy):
+    for cp in fwd_x:
         cp.wait_recv()
-    for cp in (*own_y, *own_x, own_c, fwd_x, c_y, fwd_y, c_x, c_d, a_copy):
+    c_lo = u_copy(16, d_blk, to_c, lo)
+    c_lo.start()
+    for cp in fwd_y:
+        cp.wait_recv()
+    c_hi = u_copy(17, d_blk, to_c, hi)
+    c_hi.start()
+    for cp in (own_c, c_y, c_x, c_lo, c_hi, a_copy):
+        cp.wait_recv()
+    for cp in (*own_y, *own_x, own_c, *fwd_x, c_y, *fwd_y, c_x, c_lo, c_hi, a_copy):
         cp.wait_send()
 
 
@@ -297,7 +307,7 @@
         pltpu.VMEM((half, heads, dim), F32), pltpu.VMEM((half, heads, dim), F32),
         pltpu.VMEM((heads, 128), F32), pltpu.VMEM((heads, 128), F32), pltpu.VMEM((half, heads * dim), BF16),
         pltpu.VMEM((half, d_model), BF16),
-        dma((slots,)), dma((slots,)), dma((4,)), dma((half // TB + 1,)), dma((half // TB + 1,)), dma((11,)), dma((11,)),
+        dma((slots,)), dma((slots,)), dma((4,)), dma((half // TB + 1,)), dma((half // TB + 1,)), dma((18,)), dma((18,)),
     ]
 
 
@@ -619,7 +629,7 @@
         in_specs=[vmem] * 8 + [pl.BlockSpec(memory_space=pltpu.SMEM)] + [hbm] * 6,
         out_specs=[vmem] * 3,
         scratch_shapes=[pltpu.VMEM((tokens, d_model), BF16)] + combine_scratch(args[2], args[5], args[6])
-        + attn_scratch(AHEAD, 2, tokens, kc.shape[2], kc.shape[3], wq),
+        + attn_scratch(AHEAD, 4, tokens, kc.shape[2], kc.shape[3], wq),
         compiler_params=pltpu.CompilerParams(collective_id=layer, has_side_effects=True, vmem_limit_bytes=46 << 20),
     )(*args, lens, kc, vc, wq, wk, wv, wo)
     return u.reshape(8 * half, d_model), a, a_got

time: 181 us -> 180 us (level)
  no operation moved by 1% of the time
where the time goes in v4:
time: 180 us
  Pallas kernels  151 us (84%)
  waiting for transfers between devices  21.4 us (12%)
  starting transfers between devices  4.13 us (2%)
  local copies, waits for them, and re-layouts  3.02 us (2%)
    pallas_call x6, Pallas kernels, experts(): pl.pallas_call(functools.partial(expert_kernel, layer, part), out_shape=[...  55.7 us
    pallas_call x1, Pallas kernels, next_layer(): pl.pallas_call(functools.partial(next_layer_kernel, layer), out_shape=[ja...  38.9 us
    pallas_call x1, Pallas kernels, attention(): pl.pallas_call(functools.partial(attn_kernel, layer, True), out_shape=out...  28.3 us
    ppermute x4, waiting for transfers between devices, body(): got.append(lax.ppermute(send, 'pool', [(0, 1), (1, 0)]))  21.4 us
    pallas_call x1, Pallas kernels, combine(): pl.pallas_call(combine_kernel, out_shape=jax.ShapeDtypeStruct((2 * half,...  18 us
    pallas_call x2, Pallas kernels, gates(): pl.pallas_call(functools.partial(gate_kernel, layer), out_shape=[jax.Shap...  9.95 us
    ppermute x4, starting transfers between devices, body(): got.append(lax.ppermute(send, 'pool', [(0, 1), (1, 0)]))  4.13 us
  transfers between devices with their start and end apart: 4, of which 2 were waited for; matrix products, arithmetic and copies ran while one was open for 0% of the time, Pallas kernels for 25%

profile of v4, /device:TPU:0, one launch (start us, length us, event | category | flops | bytes accessed | tf_op | source)
XLA Modules:
  0.0 179.5 jit_solution(1468199247161820266)
XLA Ops:
  0.0 0.7 copy.16
  0.7 0.0 copy-start
  0.7 0.9 copy-done
  1.7 0.0 copy-start.1
  1.7 0.7 copy-done.1
  2.3 28.3 %shard_map.127 = (bf16[8,64,1024]{2,1,0:T(8,128)(2,1)S(1)}, bf16[64,512]{1,0:T(8,128)(2,1)S(1)}, bf16[64,512]{1,0:T(8,128)(2,1)S(1)}, s32[2,8,512]{2,1,0:T(8,128...) custom-call(bf16[128,1024]{1,0:T(8,128)(2,1)S(1)} %copy-done, s32[128]{0:T(128)S(1)} %copy-done.1, ...), custom_call_target="tpu_custom_call" | custom-call | tf_op jit(solution)/shard_map/pallas_call | solution.py:332
  30.6 10.0 %shard_map.128 = (f32[384,512]{1,0:T(8,128)S(1)}, f32[384,512]{1,0:T(8,128)S(1)}) custom-call(s32[2,16,128]{2,1,0:T(8,128)S(1)} %get-tuple-element.30.off_ref, bf16[512,1024]{1,0:T(8,128)(2,1)S(1)} %bitcast.14, s32[2,8,512]{2,1,0:T(8,128)S(1)} %get-tuple-element.32.pos_ref, bf16[2,16,352,1024]{3,2,1,0:T(8,128)(2,1)} %bitcast.20, ...), custom_call_target="tpu_custom_call" | custom-call | flops 4000000000 | bytes 18874368 | tf_op jit(solution)/shard_map/pallas_call | solution.py:439
  40.7 0.4 collective-permute-start
  41.1 5.6 %shard_map.130 = (f32[256,512]{1,0:T(8,128)S(1)}, f32[256,512]{1,0:T(8,128)S(1)}) custom-call(s32[2,16,128]{2,1,0:T(8,128)S(1)} %get-tuple-element.30.off_ref, bf16[512,1024]{1,0:T(8,128)(2,1)S(1)} %bitcast.15, s32[2,8,512]{2,1,0:T(8,128)S(1)} %get-tuple-element.32.pos_ref, bf16[2,16,352,1024]{3,2,1,0:T(8,128)(2,1)} %bitcast.21, ...), custom_call_target="tpu_custom_call" | custom-call | flops 4000000000 | bytes 18874368 | tf_op jit(solution)/shard_map/pallas_call | solution.py:439
  46.7 0.0 copy-start.2
  46.7 1.7 collective-permute-start.1
  48.4 12.2 %shard_map.129 = (f32[128,512]{1,0:T(8,128)S(1)}, f32[128,512]{1,0:T(8,128)S(1)}) custom-call(s32[2,16,128]{2,1,0:T(8,128)S(1)} %get-tuple-element.30.off_ref, bf16[512,1024]{1,0:T(8,128)(2,1)S(1)} %bitcast.16, s32[2,8,512]{2,1,0:T(8,128)S(1)} %get-tuple-element.32.pos_ref, bf16[2,16,352,1024]{3,2,1,0:T(8,128)(2,1)} %bitcast.22, ...), custom_call_target="tpu_custom_call" | custom-call | flops 4000000000 | bytes 18874368 | tf_op jit(solution)/shard_map/pallas_call | solution.py:439
  60.6 10.3 %collective-permute-done.1.got_ref = f32[256,512]{1,0:T(8,128)S(1)} collective-permute-done((f32[256,512]{1,0:T(8,128)S(1)}, f32[256,512]{1,0:T(8,128)S(1)}, u32[]{:S(2)}, u32[]{:S(2)}) %collective-permute-start.1) | collective-permute-done | bytes 524320 | tf_op jit(solution)/shard_map/ppermute | solution.py:663
  70.8 0.0 copy-done.2
  70.8 5.0 %shard_map.131 = (bf16[3,512,768]{2,1,0:T(8,128)(2,1)S(1)}, f32[4,4,128,128]{3,2,1,0:T(8,128)S(1)}) custom-call(f32[256,512]{1,0:T(8,128)S(1)} %get-tuple-element.37.own_ref, f32[256,512]{1,0:T(8,128)S(1)} %collective-permute-done.1.got_ref, bf16[512,1024]{1,0:T(8,128)(2,1)S(1)} %bitcast.17, f32[2,64,1024]{2,1,0:T(8,128)S(1)} %bitcast.18, ...), custom_call_target="tpu_custom_call" | custom-call | flops 2000000000 | bytes 4194304 | tf_op jit(solution)/shard_map/pallas_call | solution.py:505
  75.8 0.0 collective-permute-done.refs_1_
  75.8 38.9 %shard_map.132 = (bf16[8,64,1024]{2,1,0:T(8,128)(2,1)S(1)}, bf16[64,512]{1,0:T(8,128)(2,1)S(1)}, bf16[64,512]{1,0:T(8,128)(2,1)S(1)}) custom-call(f32[384,512]{1,0:T(8,128)S(1)} %get-tuple-element.33.refs_0_, f32[384,512]{1,0:T(8,128)S(1)} %collective-permute-done.refs_1_, f32[128,512]{1,0:T(8,128)S(1)} %get-tuple-element.35.refs_2_, ...), custom_call_target="tpu_custom_call" | custom-call | tf_op jit(solution)/shard_map/pallas_call | solution.py:626
  114.7 10.0 %shard_map.133 = (f32[384,512]{1,0:T(8,128)S(1)}, f32[384,512]{1,0:T(8,128)S(1)}) custom-call(s32[2,16,128]{2,1,0:T(8,128)S(1)} %get-tuple-element.30.off_ref, bf16[512,1024]{1,0:T(8,128)(2,1)S(1)} %bitcast.10, s32[2,8,512]{2,1,0:T(8,128)S(1)} %get-tuple-element.32.pos_ref, bf16[2,16,352,1024]{3,2,1,0:T(8,128)(2,1)} %bitcast.23, ...), custom_call_target="tpu_custom_call" | custom-call | flops 4000000000 | bytes 18874368 | tf_op jit(solution)/shard_map/pallas_call | solution.py:439
  124.8 0.7 collective-permute-start.2
  125.4 5.8 %shard_map.135 = (f32[256,512]{1,0:T(8,128)S(1)}, f32[256,512]{1,0:T(8,128)S(1)}) custom-call(s32[2,16,128]{2,1,0:T(8,128)S(1)} %get-tuple-element.30.off_ref, bf16[512,1024]{1,0:T(8,128)(2,1)S(1)} %bitcast.11, s32[2,8,512]{2,1,0:T(8,128)S(1)} %get-tuple-element.32.pos_ref, bf16[2,16,352,1024]{3,2,1,0:T(8,128)(2,1)} %bitcast.24, ...), custom_call_target="tpu_custom_call" | custom-call | flops 4000000000 | bytes 18874368 | tf_op jit(solution)/shard_map/pallas_call | solution.py:439
  131.2 1.4 collective-permute-start.3
  132.6 12.1 %shard_map.134 = (f32[128,512]{1,0:T(8,128)S(1)}, f32[128,512]{1,0:T(8,128)S(1)}) custom-call(s32[2,16,128]{2,1,0:T(8,128)S(1)} %get-tuple-element.30.off_ref, bf16[512,1024]{1,0:T(8,128)(2,1)S(1)} %bitcast.12, s32[2,8,512]{2,1,0:T(8,128)S(1)} %get-tuple-element.32.pos_ref, bf16[2,16,352,1024]{3,2,1,0:T(8,128)(2,1)} %bitcast.25, ...), custom_call_target="tpu_custom_call" | custom-call | flops 4000000000 | bytes 18874368 | tf_op jit(solution)/shard_map/pallas_call | solution.py:439
  144.7 11.2 %collective-permute-done.3.got_ref = f32[256,512]{1,0:T(8,128)S(1)} collective-permute-done((f32[256,512]{1,0:T(8,128)S(1)}, f32[256,512]{1,0:T(8,128)S(1)}, u32[]{:S(2)}, u32[]{:S(2)}) %collective-permute-start.3) | collective-permute-done | bytes 524320 | tf_op jit(solution)/shard_map/ppermute | solution.py:663
  155.9 5.0 %shard_map.136 = (bf16[3,512,768]{2,1,0:T(8,128)(2,1)S(1)}, f32[4,4,128,128]{3,2,1,0:T(8,128)S(1)}) custom-call(f32[256,512]{1,0:T(8,128)S(1)} %get-tuple-element.49.own_ref, f32[256,512]{1,0:T(8,128)S(1)} %collective-permute-done.3.got_ref, bf16[512,1024]{1,0:T(8,128)(2,1)S(1)} %bitcast.13, f32[2,64,1024]{2,1,0:T(8,128)S(1)} %bitcast.19, ...), custom_call_target="tpu_custom_call" | custom-call | flops 2000000000 | bytes 4194304 | tf_op jit(solution)/shard_map/pallas_call | solution.py:505
  160.8 0.0 collective-permute-done.2.refs_1_
  160.9 18.0 %shard_map.137 = bf16[128,1024]{1,0:T(8,128)(2,1)S(1)} custom-call(f32[384,512]{1,0:T(8,128)S(1)} %get-tuple-element.45.refs_0_, f32[384,512]{1,0:T(8,128)S(1)} %collective-permute-done.2.refs_1_, f32[128,512]{1,0:T(8,128)S(1)} %get-tuple-element.47.refs_2_, f32[128,512]{1,0:T(8,128)S(1)} %get-tuple-element.48.refs_3_, ...), custom_call_target="tpu_custom_call" | custom-call | tf_op jit(solution)/shard_map/pallas_call | solution.py:611
  178.8 0.7 copy.18
  (1 shorter events, 0.0 us)
Async XLA Ops:
  0.7 0.9 copy-start
  1.7 0.7 copy-start.1
  40.7 35.1 %collective-permute-start = (f32[384,512]{1,0:T(8,128)S(1)}, f32[384,512]{1,0:T(8,128)S(1)}, u32[]{:S(2)}, u32[]{:S(2)}) collective-permute-start(f32[384,512]{1,0:T(8,128)S(1)} %get-tuple-element.34), channel_id=1, source_target_pairs={{0,4},{4,0},{1,5},{5,1},{2,6},{6,2},{3,7},{7,3}} | collective-permute-start | bytes 2359304 | tf_op jit(solution)/shard_map/ppermute | solution.py:663
  46.7 24.2 %copy-start.2 = (f32[2,1024,64]{1,2,0:T(8,128)S(1)}, f32[2,1024,64]{1,2,0:T(8,128)}, u32[]{:S(2)}) copy-start(f32[2,1024,64]{1,2,0:T(8,128)} %param.21) | copy-start | bytes 1572868
  46.7 24.2 %collective-permute-start.1 = (f32[256,512]{1,0:T(8,128)S(1)}, f32[256,512]{1,0:T(8,128)S(1)}, u32[]{:S(2)}, u32[]{:S(2)}) collective-permute-start(f32[256,512]{1,0:T(8,128)S(1)} %get-tuple-element.38), channel_id=1, source_target_pairs={{0,4},{4,0},{1,5},{5,1},{2,6},{6,2},{3,7},{7,3}} | collective-permute-start | bytes 1572872 | tf_op jit(solution)/shard_map/ppermute | solution.py:663
  124.8 36.1 %collective-permute-start.2 = (f32[384,512]{1,0:T(8,128)S(1)}, f32[384,512]{1,0:T(8,128)S(1)}, u32[]{:S(2)}, u32[]{:S(2)}) collective-permute-start(f32[384,512]{1,0:T(8,128)S(1)} %get-tuple-element.46), channel_id=1, source_target_pairs={{0,4},{4,0},{1,5},{5,1},{2,6},{6,2},{3,7},{7,3}} | collective-permute-start | bytes 2359304 | tf_op jit(solution)/shard_map/ppermute | solution.py:663
  131.2 24.6 %collective-permute-start.3 = (f32[256,512]{1,0:T(8,128)S(1)}, f32[256,512]{1,0:T(8,128)S(1)}, u32[]{:S(2)}, u32[]{:S(2)}) collective-permute-start(f32[256,512]{1,0:T(8,128)S(1)} %get-tuple-element.50), channel_id=1, source_target_pairs={{0,4},{4,0},{1,5},{5,1},{2,6},{6,2},{3,7},{7,3}} | collective-permute-start | bytes 1572872 | tf_op jit(solution)/shard_map/ppermute | solution.py:663

commit v5 on v4

--- a/solution.py
+++ b/solution.py
@@ -162,9 +162,10 @@
                 for j in range(TB):
                     q = q3[t0 + j].astype(BF16)
                     s = _nt(q, kbuf[n % slots, j])
-                    s = jnp.where(posl < len_ref[t0 + j], s * scale, NEG)
+                    seen = posl < len_ref[t0 + j]
+                    s = jnp.where(seen, s * scale, NEG)
                     m = jnp.max(s, axis=1, keepdims=True)
-                    pr = jnp.exp(s - m)
+                    pr = jnp.where(seen, jnp.exp(s - m), 0.0)
                     l = jnp.sum(pr, axis=1, keepdims=True)
                     pbuf[g * TB + j] = pr.astype(BF16)
                     at = (n % n_half) * TB + j

time: 180 us -> 180 us (level)
  no operation moved by 1% of the time
where the time goes in v5:
time: 180 us
  Pallas kernels  151 us (84%)
  waiting for transfers between devices  21.4 us (12%)
  starting transfers between devices  4.12 us (2%)
  local copies, waits for them, and re-layouts  3.02 us (2%)
    pallas_call x6, Pallas kernels, experts(): pl.pallas_call(functools.partial(expert_kernel, layer, part), out_shape=[...  55.7 us
    pallas_call x1, Pallas kernels, next_layer(): pl.pallas_call(functools.partial(next_layer_kernel, layer), out_shape=[ja...  38.9 us
    pallas_call x1, Pallas kernels, attention(): pl.pallas_call(functools.partial(attn_kernel, layer, True), out_shape=out...  28.3 us
    ppermute x4, waiting for transfers between devices, body(): got.append(lax.ppermute(send, 'pool', [(0, 1), (1, 0)]))  21.4 us
    pallas_call x1, Pallas kernels, combine(): pl.pallas_call(combine_kernel, out_shape=jax.ShapeDtypeStruct((2 * half,...  18 us
    pallas_call x2, Pallas kernels, gates(): pl.pallas_call(functools.partial(gate_kernel, layer), out_shape=[jax.Shap...  9.95 us
    ppermute x4, starting transfers between devices, body(): got.append(lax.ppermute(send, 'pool', [(0, 1), (1, 0)]))  4.12 us
  transfers between devices with their start and end apart: 4, of which 2 were waited for; matrix products, arithmetic and copies ran while one was open for 0% of the time, Pallas kernels for 25%

profile of v5, /device:TPU:0, one launch (start us, length us, event | category | flops | bytes accessed | tf_op | source)
XLA Modules:
  0.0 179.5 jit_solution(9164562925930109193)
XLA Ops:
  0.0 0.7 copy.16
  0.7 0.0 copy-start
  0.7 0.9 copy-done
  1.7 0.0 copy-start.1
  1.7 0.7 copy-done.1
  2.3 28.3 %shard_map.127 = (bf16[8,64,1024]{2,1,0:T(8,128)(2,1)S(1)}, bf16[64,512]{1,0:T(8,128)(2,1)S(1)}, bf16[64,512]{1,0:T(8,128)(2,1)S(1)}, s32[2,8,512]{2,1,0:T(8,128...) custom-call(bf16[128,1024]{1,0:T(8,128)(2,1)S(1)} %copy-done, s32[128]{0:T(128)S(1)} %copy-done.1, ...), custom_call_target="tpu_custom_call" | custom-call | tf_op jit(solution)/shard_map/pallas_call | solution.py:333
  30.6 10.0 %shard_map.128 = (f32[384,512]{1,0:T(8,128)S(1)}, f32[384,512]{1,0:T(8,128)S(1)}) custom-call(s32[2,16,128]{2,1,0:T(8,128)S(1)} %get-tuple-element.30.off_ref, bf16[512,1024]{1,0:T(8,128)(2,1)S(1)} %bitcast.14, s32[2,8,512]{2,1,0:T(8,128)S(1)} %get-tuple-element.32.pos_ref, bf16[2,16,352,1024]{3,2,1,0:T(8,128)(2,1)} %bitcast.20, ...), custom_call_target="tpu_custom_call" | custom-call | flops 4000000000 | bytes 18874368 | tf_op jit(solution)/shard_map/pallas_call | solution.py:440
  40.7 0.4 collective-permute-start
  41.0 5.6 %shard_map.130 = (f32[256,512]{1,0:T(8,128)S(1)}, f32[256,512]{1,0:T(8,128)S(1)}) custom-call(s32[2,16,128]{2,1,0:T(8,128)S(1)} %get-tuple-element.30.off_ref, bf16[512,1024]{1,0:T(8,128)(2,1)S(1)} %bitcast.15, s32[2,8,512]{2,1,0:T(8,128)S(1)} %get-tuple-element.32.pos_ref, bf16[2,16,352,1024]{3,2,1,0:T(8,128)(2,1)} %bitcast.21, ...), custom_call_target="tpu_custom_call" | custom-call | flops 4000000000 | bytes 18874368 | tf_op jit(solution)/shard_map/pallas_call | solution.py:440
  46.7 0.0 copy-start.2
  46.7 1.7 collective-permute-start.1
  48.4 12.2 %shard_map.129 = (f32[128,512]{1,0:T(8,128)S(1)}, f32[128,512]{1,0:T(8,128)S(1)}) custom-call(s32[2,16,128]{2,1,0:T(8,128)S(1)} %get-tuple-element.30.off_ref, bf16[512,1024]{1,0:T(8,128)(2,1)S(1)} %bitcast.16, s32[2,8,512]{2,1,0:T(8,128)S(1)} %get-tuple-element.32.pos_ref, bf16[2,16,352,1024]{3,2,1,0:T(8,128)(2,1)} %bitcast.22, ...), custom_call_target="tpu_custom_call" | custom-call | flops 4000000000 | bytes 18874368 | tf_op jit(solution)/shard_map/pallas_call | solution.py:440
  60.6 10.3 %collective-permute-done.1.got_ref = f32[256,512]{1,0:T(8,128)S(1)} collective-permute-done((f32[256,512]{1,0:T(8,128)S(1)}, f32[256,512]{1,0:T(8,128)S(1)}, u32[]{:S(2)}, u32[]{:S(2)}) %collective-permute-start.1) | collective-permute-done | bytes 524320 | tf_op jit(solution)/shard_map/ppermute | solution.py:664
  70.8 0.0 copy-done.2
  70.8 5.0 %shard_map.131 = (bf16[3,512,768]{2,1,0:T(8,128)(2,1)S(1)}, f32[4,4,128,128]{3,2,1,0:T(8,128)S(1)}) custom-call(f32[256,512]{1,0:T(8,128)S(1)} %get-tuple-element.37.own_ref, f32[256,512]{1,0:T(8,128)S(1)} %collective-permute-done.1.got_ref, bf16[512,1024]{1,0:T(8,128)(2,1)S(1)} %bitcast.17, f32[2,64,1024]{2,1,0:T(8,128)S(1)} %bitcast.18, ...), custom_call_target="tpu_custom_call" | custom-call | flops 2000000000 | bytes 4194304 | tf_op jit(solution)/shard_map/pallas_call | solution.py:506
  75.8 0.0 collective-permute-done.refs_1_
  75.8 38.9 %shard_map.132 = (bf16[8,64,1024]{2,1,0:T(8,128)(2,1)S(1)}, bf16[64,512]{1,0:T(8,128)(2,1)S(1)}, bf16[64,512]{1,0:T(8,128)(2,1)S(1)}) custom-call(f32[384,512]{1,0:T(8,128)S(1)} %get-tuple-element.33.refs_0_, f32[384,512]{1,0:T(8,128)S(1)} %collective-permute-done.refs_1_, f32[128,512]{1,0:T(8,128)S(1)} %get-tuple-element.35.refs_2_, ...), custom_call_target="tpu_custom_call" | custom-call | tf_op jit(solution)/shard_map/pallas_call | solution.py:627
  114.7 10.0 %shard_map.133 = (f32[384,512]{1,0:T(8,128)S(1)}, f32[384,512]{1,0:T(8,128)S(1)}) custom-call(s32[2,16,128]{2,1,0:T(8,128)S(1)} %get-tuple-element.30.off_ref, bf16[512,1024]{1,0:T(8,128)(2,1)S(1)} %bitcast.10, s32[2,8,512]{2,1,0:T(8,128)S(1)} %get-tuple-element.32.pos_ref, bf16[2,16,352,1024]{3,2,1,0:T(8,128)(2,1)} %bitcast.23, ...), custom_call_target="tpu_custom_call" | custom-call | flops 4000000000 | bytes 18874368 | tf_op jit(solution)/shard_map/pallas_call | solution.py:440
  124.7 0.7 collective-permute-start.2
  125.4 5.8 %shard_map.135 = (f32[256,512]{1,0:T(8,128)S(1)}, f32[256,512]{1,0:T(8,128)S(1)}) custom-call(s32[2,16,128]{2,1,0:T(8,128)S(1)} %get-tuple-element.30.off_ref, bf16[512,1024]{1,0:T(8,128)(2,1)S(1)} %bitcast.11, s32[2,8,512]{2,1,0:T(8,128)S(1)} %get-tuple-element.32.pos_ref, bf16[2,16,352,1024]{3,2,1,0:T(8,128)(2,1)} %bitcast.24, ...), custom_call_target="tpu_custom_call" | custom-call | flops 4000000000 | bytes 18874368 | tf_op jit(solution)/shard_map/pallas_call | solution.py:440
  131.2 1.4 collective-permute-start.3
  132.6 12.1 %shard_map.134 = (f32[128,512]{1,0:T(8,128)S(1)}, f32[128,512]{1,0:T(8,128)S(1)}) custom-call(s32[2,16,128]{2,1,0:T(8,128)S(1)} %get-tuple-element.30.off_ref, bf16[512,1024]{1,0:T(8,128)(2,1)S(1)} %bitcast.12, s32[2,8,512]{2,1,0:T(8,128)S(1)} %get-tuple-element.32.pos_ref, bf16[2,16,352,1024]{3,2,1,0:T(8,128)(2,1)} %bitcast.25, ...), custom_call_target="tpu_custom_call" | custom-call | flops 4000000000 | bytes 18874368 | tf_op jit(solution)/shard_map/pallas_call | solution.py:440
  144.7 11.1 %collective-permute-done.3.got_ref = f32[256,512]{1,0:T(8,128)S(1)} collective-permute-done((f32[256,512]{1,0:T(8,128)S(1)}, f32[256,512]{1,0:T(8,128)S(1)}, u32[]{:S(2)}, u32[]{:S(2)}) %collective-permute-start.3) | collective-permute-done | bytes 524320 | tf_op jit(solution)/shard_map/ppermute | solution.py:664
  155.9 5.0 %shard_map.136 = (bf16[3,512,768]{2,1,0:T(8,128)(2,1)S(1)}, f32[4,4,128,128]{3,2,1,0:T(8,128)S(1)}) custom-call(f32[256,512]{1,0:T(8,128)S(1)} %get-tuple-element.49.own_ref, f32[256,512]{1,0:T(8,128)S(1)} %collective-permute-done.3.got_ref, bf16[512,1024]{1,0:T(8,128)(2,1)S(1)} %bitcast.13, f32[2,64,1024]{2,1,0:T(8,128)S(1)} %bitcast.19, ...), custom_call_target="tpu_custom_call" | custom-call | flops 2000000000 | bytes 4194304 | tf_op jit(solution)/shard_map/pallas_call | solution.py:506
  160.8 0.0 collective-permute-done.2.refs_1_
  160.8 18.0 %shard_map.137 = bf16[128,1024]{1,0:T(8,128)(2,1)S(1)} custom-call(f32[384,512]{1,0:T(8,128)S(1)} %get-tuple-element.45.refs_0_, f32[384,512]{1,0:T(8,128)S(1)} %collective-permute-done.2.refs_1_, f32[128,512]{1,0:T(8,128)S(1)} %get-tuple-element.47.refs_2_, f32[128,512]{1,0:T(8,128)S(1)} %get-tuple-element.48.refs_3_, ...), custom_call_target="tpu_custom_call" | custom-call | tf_op jit(solution)/shard_map/pallas_call | solution.py:612
  178.8 0.7 copy.18
  (1 shorter events, 0.0 us)
Async XLA Ops:
  0.7 0.9 copy-start
  1.7 0.7 copy-start.1
  40.7 35.1 %collective-permute-start = (f32[384,512]{1,0:T(8,128)S(1)}, f32[384,512]{1,0:T(8,128)S(1)}, u32[]{:S(2)}, u32[]{:S(2)}) collective-permute-start(f32[384,512]{1,0:T(8,128)S(1)} %get-tuple-element.34), channel_id=1, source_target_pairs={{0,4},{4,0},{1,5},{5,1},{2,6},{6,2},{3,7},{7,3}} | collective-permute-start | bytes 2359304 | tf_op jit(solution)/shard_map/ppermute | solution.py:664
  46.7 24.2 %copy-start.2 = (f32[2,1024,64]{1,2,0:T(8,128)S(1)}, f32[2,1024,64]{1,2,0:T(8,128)}, u32[]{:S(2)}) copy-start(f32[2,1024,64]{1,2,0:T(8,128)} %param.21) | copy-start | bytes 1572868
  46.7 24.2 %collective-permute-start.1 = (f32[256,512]{1,0:T(8,128)S(1)}, f32[256,512]{1,0:T(8,128)S(1)}, u32[]{:S(2)}, u32[]{:S(2)}) collective-permute-start(f32[256,512]{1,0:T(8,128)S(1)} %get-tuple-element.38), channel_id=1, source_target_pairs={{0,4},{4,0},{1,5},{5,1},{2,6},{6,2},{3,7},{7,3}} | collective-permute-start | bytes 1572872 | tf_op jit(solution)/shard_map/ppermute | solution.py:664
  124.7 36.1 %collective-permute-start.2 = (f32[384,512]{1,0:T(8,128)S(1)}, f32[384,512]{1,0:T(8,128)S(1)}, u32[]{:S(2)}, u32[]{:S(2)}) collective-permute-start(f32[384,512]{1,0:T(8,128)S(1)} %get-tuple-element.46), channel_id=1, source_target_pairs={{0,4},{4,0},{1,5},{5,1},{2,6},{6,2},{3,7},{7,3}} | collective-permute-start | bytes 2359304 | tf_op jit(solution)/shard_map/ppermute | solution.py:664
  131.2 24.6 %collective-permute-start.3 = (f32[256,512]{1,0:T(8,128)S(1)}, f32[256,512]{1,0:T(8,128)S(1)}, u32[]{:S(2)}, u32[]{:S(2)}) collective-permute-start(f32[256,512]{1,0:T(8,128)S(1)} %get-tuple-element.50), channel_id=1, source_target_pairs={{0,4},{4,0},{1,5},{5,1},{2,6},{6,2},{3,7},{7,3}} | collective-permute-start | bytes 1572872 | tf_op jit(solution)/shard_map/ppermute | solution.py:664
